TPU v7x, 128 devices: a whole 4x4x4 slice. The times are simulated.
128 devices in a mesh: row: 4 (over y), col: 32 (over z, x, core).
Axes of the slice: x: 4, y: 4, z: 4, core: 2. Of those that a mesh axis runs over, the one named last changes fastest.
Arguments:
- node_features: bfloat16 [8192, 128, 512], P(('row', 'col')), may hold values from -6 to 6
- node_counts: int32 [8192], P(('row', 'col')), may hold values from 16 to 128, as said below
- edge_list: int32 [8192, 2, 256], P(('row', 'col')), may hold values from 0 to 128, as said below
- readout_ids: int32 [8192], P(('row', 'col')), may hold values from 0 to 1023
- live_graphs: int32 [128], P(('row', 'col')), may hold values from 1 to 64, as said below
- self_weight: float32 [1], replicated, may hold values from 0.5 to 1.5
- w_first: bfloat16 [512, 512], replicated, may hold values from -0.25 to 0.25
- b_first: float32 [512], replicated, may hold values from -3 to 3
- w_second: bfloat16 [512, 512], replicated, may hold values from -0.25 to 0.25
- b_second: float32 [512], replicated, may hold values from -3 to 3
- w_third: bfloat16 [512, 512], replicated, may hold values from -0.25 to 0.25
- b_third: float32 [512], replicated, may hold values from -3 to 3
Outputs:
- node_out: bfloat16 [4096, 128, 512], P(('row', 'col'))
- readout: float32 [1024, 512], P(('row', 'col'))
Inputs may be any that keep to these rules, and one draw needn't show every extreme that they name: `live_graphs`: the entries sum to 4096, and at least one equals 64. `node_counts`: node slots 0 to count - 1 of a graph are live; the rest of its block is padding. `edge_list`: each edge slot holds two node indices below its graph's node count, or 128 in both rows for an unused slot.
All inputs are finite; a program needn't handle non-finite values.
Results may differ from a plain program's by a relative error of at most 0.0058.
Values may be sent and summed in bfloat16 or wider, within the bound.
No kernel may reach another device: no remote copies, remote signals or barrier semaphores. Data moves between devices by JAX's collectives and lax.ppermute only.
A program may use at most 128 MiB of HBM per device.

v0:
```python
import jax
import jax.numpy as jnp
from jax import lax
from jax.experimental import pallas as pl
from jax.experimental.pallas import tpu as pltpu
from jax.sharding import Mesh
from jax.sharding import PartitionSpec as P

G_DEV = 32
READ_DEV = 8
ROW_COL = ("row", "col_0", "col_1", "col_2")
CHIP = ("row", "col_0", "col_1")
SWAP = [(0, 1), (1, 0)]
PACK_BITS = 3
PACK = 1 << PACK_BITS
POOL = 8
MLP_BITS = 2
HEAD_ROWS = 112
TAIL_GRAPHS = 16
MLP = 1 << MLP_BITS
VMEM_BYTES = 58 * 1024 * 1024
FINISH_BYTES = 24 * 1024 * 1024


def masked_sum(keep, values, axis):
    return jnp.sum(jnp.where(keep, values, 0), axis=axis)


def blend_kernel(
    where, scale, own, par, own_edges, par_edges, head, tail, taken, made, taken_sem, made_sem
):
    core, offset, live_a, live_b = where[0], where[1], where[2], where[3]
    count, nodes, _ = taken.shape
    wrap = 2 * count - 1
    node_index = lax.broadcasted_iota(jnp.int32, (nodes, own_edges.shape[-1]), 0)

    def source_of(slot):
        number = (2 * slot + core - offset) & wrap
        filled = number < live_a + live_b
        from_b = number >= live_a
        index = jnp.where(filled, jnp.where(from_b, number - live_a, number), slot)
        return index, jnp.logical_xor(from_b, core == 1)

    @pl.loop(0, count)
    def _(slot):
        index, from_par = source_of(slot)
        sem = taken_sem.at[slot >> PACK_BITS]

        @pl.when(from_par)
        def _():
            pltpu.make_async_copy(par.at[index], taken.at[slot], sem).start()

        @pl.when(jnp.logical_not(from_par))
        def _():
            pltpu.make_async_copy(own.at[index], taken.at[slot], sem).start()

    cuts = ((head, pl.ds(0, HEAD_ROWS)), (tail, pl.ds(HEAD_ROWS, nodes - HEAD_ROWS)))

    def put(group, which):
        rows = pl.ds(group * PACK, PACK)
        out, cut = cuts[which]
        return pltpu.make_async_copy(made.at[rows, cut], out.at[rows], made_sem.at[which, group])

    @pl.loop(0, count // PACK)
    def _(group):
        pltpu.make_async_copy(
            own.at[pl.ds(0, PACK)], taken.at[pl.ds(group * PACK, PACK)], taken_sem.at[group]
        ).wait()
        slots = [group * PACK + lane for lane in range(PACK)]
        sources, targets = [], []
        for slot in slots:
            index, from_par = source_of(slot)
            edges = jnp.where(from_par, par_edges[index], own_edges[index])
            sources.append((node_index == edges[0:1, :]).astype(jnp.bfloat16))
            targets.append((node_index == edges[1:2, :]).astype(jnp.bfloat16))
        adjacency = [
            lax.dot_general(t, s, (((1,), (1,)), ((), ())), preferred_element_type=jnp.float32)
            for t, s in zip(targets, sources)
        ]
        features = [taken[slot] for slot in slots]
        neighbours = [
            jnp.dot(a.astype(jnp.bfloat16), f, preferred_element_type=jnp.float32)
            for a, f in zip(adjacency, features)
        ]
        for slot, f, n in zip(slots, features, neighbours):
            made[slot] = (scale[0] * f.astype(jnp.float32) + n).astype(jnp.bfloat16)
        put(group, 0).start()
        put(group, 1).start()

    @pl.loop(0, count // PACK)
    def _(group):
        put(group, 0).wait()
        put(group, 1).wait()


def blended_slots(own, par, own_edges, par_edges, where, scale):
    count, nodes, hidden = own.shape
    anywhere = pl.BlockSpec(memory_space=pl.ANY)
    vector = pl.BlockSpec(memory_space=pltpu.VMEM)
    scalar = pl.BlockSpec(memory_space=pltpu.SMEM)
    return pl.pallas_call(
        blend_kernel,
        out_shape=[
            jax.ShapeDtypeStruct((count, rows, hidden), jnp.bfloat16)
            for rows in (HEAD_ROWS, nodes - HEAD_ROWS)
        ],
        in_specs=[scalar, scalar, anywhere, anywhere, vector, vector],
        out_specs=[anywhere, anywhere],
        scratch_shapes=[
            pltpu.VMEM((count, nodes, hidden), jnp.bfloat16),
            pltpu.VMEM((count, nodes, hidden), jnp.bfloat16),
            pltpu.SemaphoreType.DMA((count // PACK,)),
            pltpu.SemaphoreType.DMA((2, count // PACK)),
        ],
        compiler_params=pltpu.CompilerParams(vmem_limit_bytes=VMEM_BYTES),
        cost_estimate=pl.CostEstimate(
            flops=2 * count * nodes * nodes * (own_edges.shape[-1] + hidden),
            bytes_accessed=4 * count * nodes * hidden,
            transcendentals=0,
        ),
        name="blend",
    )(where, scale, own, par, own_edges, par_edges)


def perceptron(rows, weights):
    w_first, b_first, w_second, b_second, w_third, b_third = weights
    for w, b in ((w_first, b_first), (w_second, b_second)):
        total = jnp.dot(rows, w[...], preferred_element_type=jnp.float32) + b[...]
        rows = jnp.maximum(total, 0.0).astype(jnp.bfloat16)
    return jnp.dot(rows, w_third[...], preferred_element_type=jnp.float32) + b_third[...]


def weight_specs(weights):
    return [pl.BlockSpec(w.shape, lambda i, *tables: (0, 0)) for w in weights]


def mlp_cost(rows, hidden):
    return pl.CostEstimate(
        flops=6 * rows * hidden * hidden, bytes_accessed=4 * rows * hidden, transcendentals=0
    )


def pool_kernel(counts, head_ref, tail_ref, *refs):
    weights, out = refs[:6], refs[6]
    step = pl.program_id(0)
    many, head, hidden = head_ref.shape
    tail = tail_ref.shape[1]
    rows = jnp.concatenate(
        [head_ref[...].reshape(many * head, hidden), tail_ref[...].reshape(many * tail, hidden)],
        axis=0,
    )
    result = perceptron(rows, weights)
    for lane in range(many):
        count = counts[step * many + lane]
        total = jnp.zeros((1, hidden), jnp.float32)
        for first, start, size in ((0, lane * head, head), (head, many * head + lane * tail, tail)):
            node_index = first + lax.broadcasted_iota(jnp.int32, (size, 1), 0)
            kept = jnp.where(node_index < count, result[start : start + size], 0.0)
            kept = kept.astype(jnp.bfloat16).astype(jnp.float32)
            total = total + jnp.sum(kept, axis=0, keepdims=True)
        out[lane : lane + 1, :] = total / jnp.maximum(count, 1).astype(jnp.float32)


def pooled_slots(heads, tails, counts, weights):
    count, head, hidden = heads.shape
    tail = tails.shape[1]
    return pl.pallas_call(
        pool_kernel,
        out_shape=jax.ShapeDtypeStruct((count, hidden), jnp.float32),
        grid_spec=pltpu.PrefetchScalarGridSpec(
            num_scalar_prefetch=1,
            grid=(count // POOL,),
            in_specs=[
                pl.BlockSpec((POOL, head, hidden), lambda i, *tables: (i, 0, 0)),
                pl.BlockSpec((POOL, tail, hidden), lambda i, *tables: (i, 0, 0)),
            ]
            + weight_specs(weights),
            out_specs=pl.BlockSpec((POOL, hidden), lambda i, *tables: (i, 0)),
        ),
        compiler_params=pltpu.CompilerParams(dimension_semantics=("arbitrary",)),
        cost_estimate=mlp_cost(count * (head + tail), hidden),
        name="pool",
    )(counts, heads, tails, *weights)


def place_kernel(chips, counts, arrived, *refs):
    weights, out, taken, made, taken_sem, made_sem = refs[:6], *refs[6:]
    count, nodes, hidden = taken.shape

    @pl.loop(0, count)
    def _(slot):
        pltpu.make_async_copy(
            arrived.at[chips[slot]], taken.at[slot], taken_sem.at[slot >> MLP_BITS]
        ).start()

    def put(group):
        rows = pl.ds(group * MLP, MLP)
        return pltpu.make_async_copy(
            made.at[rows], out.at[rows, pl.ds(0, nodes)], made_sem.at[group]
        )

    node_index = lax.broadcasted_iota(jnp.int32, (nodes, 1), 0)

    @pl.loop(0, count // MLP)
    def _(group):
        rows = pl.ds(group * MLP, MLP)
        pltpu.make_async_copy(
            arrived.at[pl.ds(0, MLP)], taken.at[rows], taken_sem.at[group]
        ).wait()
        result = perceptron(taken[rows].reshape(MLP * nodes, hidden), weights)
        for lane in range(MLP):
            slot = group * MLP + lane
            part = result[lane * nodes : (lane + 1) * nodes]
            made[slot] = jnp.where(node_index < counts[slot], part, 0.0).astype(jnp.bfloat16)
        put(group).start()

    @pl.loop(0, count // MLP)
    def _(group):
        put(group).wait()


def placed_heads(arrived, chips, counts, weights, nodes):
    _, head, hidden = arrived.shape
    anywhere = pl.BlockSpec(memory_space=pl.ANY)
    vector = pl.BlockSpec(memory_space=pltpu.VMEM)
    scalar = pl.BlockSpec(memory_space=pltpu.SMEM)
    return pl.pallas_call(
        place_kernel,
        out_shape=jax.ShapeDtypeStruct((G_DEV, nodes, hidden), jnp.bfloat16),
        in_specs=[scalar, scalar, anywhere] + [vector] * 6,
        out_specs=anywhere,
        scratch_shapes=[
            pltpu.VMEM((G_DEV, head, hidden), jnp.bfloat16),
            pltpu.VMEM((G_DEV, head, hidden), jnp.bfloat16),
            pltpu.SemaphoreType.DMA((G_DEV // MLP,)),
            pltpu.SemaphoreType.DMA((G_DEV // MLP,)),
        ],
        compiler_params=pltpu.CompilerParams(vmem_limit_bytes=VMEM_BYTES),
        cost_estimate=mlp_cost(G_DEV * head, hidden),
        name="place",
    )(chips, counts, arrived, *weights)


def finish_kernel(chips, counts, arrived, *refs):
    weights, (_, out, readout, made, made_sem) = refs[:6], refs[6:]
    count, tail, hidden = made.shape
    nodes = out.shape[1]

    def put(group):
        rows = pl.ds(group * TAIL_GRAPHS, TAIL_GRAPHS)
        return pltpu.make_async_copy(
            made.at[rows], out.at[rows, pl.ds(nodes - tail, tail)], made_sem.at[group]
        )

    node_index = nodes - tail + lax.broadcasted_iota(jnp.int32, (tail, 1), 0)
    for group in range(count // TAIL_GRAPHS):
        slots = [group * TAIL_GRAPHS + lane for lane in range(TAIL_GRAPHS)]
        rows = jnp.concatenate([arrived[chips[slot], :tail] for slot in slots], axis=0)
        result = perceptron(rows, weights)
        for lane, slot in enumerate(slots):
            part = result[lane * tail : (lane + 1) * tail]
            made[slot] = jnp.where(node_index < counts[slot], part, 0.0).astype(jnp.bfloat16)
        put(group).start()
    readout[...] = jnp.sum(arrived[:, tail:].astype(jnp.float32), axis=0)
    for group in range(count // TAIL_GRAPHS):
        put(group).wait()


def finished(node_out, arrived, chips, counts, weights):
    count, nodes, hidden = node_out.shape
    tail = arrived.shape[1] - READ_DEV
    anywhere = pl.BlockSpec(memory_space=pl.ANY)
    vector = pl.BlockSpec(memory_space=pltpu.VMEM)
    scalar = pl.BlockSpec(memory_space=pltpu.SMEM)
    return pl.pallas_call(
        finish_kernel,
        out_shape=[
            jax.ShapeDtypeStruct(node_out.shape, jnp.bfloat16),
            jax.ShapeDtypeStruct((READ_DEV, hidden), jnp.float32),
        ],
        in_specs=[scalar, scalar, vector] + [vector] * 6 + [anywhere],
        out_specs=[anywhere, vector],
        scratch_shapes=[
            pltpu.VMEM((count, tail, hidden), jnp.bfloat16),
            pltpu.SemaphoreType.DMA((count // TAIL_GRAPHS,)),
        ],
        input_output_aliases={9: 0},
        compiler_params=pltpu.CompilerParams(vmem_limit_bytes=FINISH_BYTES),
        cost_estimate=mlp_cost(count * tail, hidden),
        name="finish",
    )(chips, counts, arrived, *weights, node_out)


def body(
    node_features,
    node_counts,
    edge_list,
    readout_ids,
    live_graphs,
    self_weight,
    w_first,
    b_first,
    w_second,
    b_second,
    w_third,
    b_third,
):
    weights = (
        w_first,
        b_first[None, :],
        w_second,
        b_second[None, :],
        w_third,
        b_third[None, :],
    )
    devices = lax.axis_size(ROW_COL)
    capacity, nodes, hidden = node_features.shape
    me = lax.axis_index(ROW_COL)
    core = lax.axis_index("col_2")
    chip = lax.axis_index(CHIP)

    par_features = lax.ppermute(node_features, "col_2", SWAP)
    par_edges = lax.ppermute(edge_list, "col_2", SWAP)
    info = jnp.concatenate([live_graphs, node_counts, readout_ids])
    table = lax.all_to_all(
        jnp.broadcast_to(info[None], (devices, info.shape[0])), ROW_COL, 0, 0, tiled=True
    )
    live = table[:, 0]

    device = lax.broadcasted_iota(jnp.int32, (4, devices), 1)
    part = lax.broadcasted_iota(jnp.int32, (4, devices), 0)
    ahead = (part == 1) & (device < 2 * chip)
    mine = (part >= 2) & (device == 2 * chip + part - 2)
    own = (part == 0) & (device < core)
    place = masked_sum(ahead | mine | own, jnp.where(own, 1, live[None, :]), 1)

    heads, tails = blended_slots(
        node_features, par_features, edge_list, par_edges, place, self_weight
    )
    arrived = lax.all_to_all(heads, CHIP, split_axis=0, concat_axis=0, tiled=True)

    offset, live_a, live_b = place[1], place[2], place[3]
    slot = lax.broadcasted_iota(jnp.int32, (devices // 2,), 0)
    number = (2 * slot + core - offset) & (devices - 1)
    filled = number < live_a + live_b
    picked = jnp.where(number >= live_a, capacity + number - live_a, number)
    pair = lax.dynamic_slice_in_dim(table, 2 * chip, 2, 0)
    spot = lax.broadcasted_iota(jnp.int32, (devices // 2, 2 * capacity), 1) == picked[:, None]
    spot = spot & filled[:, None]
    slot_counts = masked_sum(spot, pair[:, 1 : 1 + capacity].reshape(1, -1), 1)
    slot_ids = masked_sum(spot, pair[:, 1 + capacity :].reshape(1, -1), 1)
    slot_ids = jnp.where(filled, slot_ids, -1)
    pooled = pooled_slots(heads, tails, slot_counts, weights)
    groups = READ_DEV * devices
    id_keys = lax.broadcasted_iota(jnp.int32, (groups, slot_ids.shape[0]), 0)
    members = (id_keys == slot_ids[None, :]).astype(jnp.float32)
    terms = jnp.dot(
        members, pooled, precision=lax.Precision.HIGHEST, preferred_element_type=jnp.float32
    )
    terms = terms.reshape(devices // 2, 2, READ_DEV, hidden)
    kept = lax.dynamic_index_in_dim(terms, core, 1, keepdims=False)
    sent = lax.dynamic_index_in_dim(terms, 1 - core, 1, keepdims=False).astype(jnp.bfloat16)
    both = kept + lax.ppermute(sent, "col_2", SWAP).astype(jnp.float32)
    rest = jnp.concatenate([tails, both.astype(jnp.bfloat16)], axis=1)
    rest, arrived = lax.optimization_barrier((rest, arrived))
    arrived_rest = lax.all_to_all(rest, CHIP, split_axis=0, concat_axis=0, tiled=True)

    order = lax.broadcasted_iota(jnp.int32, (G_DEV, 1), 0) * devices + me
    shape = (devices, devices)
    before = lax.broadcasted_iota(jnp.int32, shape, 1) <= lax.broadcasted_iota(jnp.int32, shape, 0)
    upto = masked_sum(before, live[None, :], 1)
    passed = upto[None, :] <= order
    source = jnp.sum(passed.astype(jnp.int32), axis=1)
    start = jnp.max(jnp.where(passed, upto[None, :], 0), axis=1)
    source_idx = order[:, 0] - start
    every = lax.broadcasted_iota(jnp.int32, (devices,), 0)
    hit = (every[None, :, None] == source[:, None, None]) & (
        lax.broadcasted_iota(jnp.int32, (1, 1, capacity), 2) == source_idx[:, None, None]
    )
    counts = jnp.sum(jnp.where(hit, table[None, :, 1 : 1 + capacity], 0), axis=(1, 2))
    chips = source >> 1
    node_out = placed_heads(arrived, chips, counts, weights, nodes)
    return tuple(finished(node_out, arrived_rest, chips, counts, weights))


def solution(mesh):
    split = Mesh(
        mesh.devices.reshape(mesh.shape["row"], 4, 4, 2), ("row", "col_0", "col_1", "col_2")
    )
    return jax.shard_map(
        body,
        mesh=split,
        in_specs=(
            P(ROW_COL, None, None),
            P(ROW_COL),
            P(ROW_COL, None, None),
            P(ROW_COL),
            P(ROW_COL),
            P(),
            P(),
            P(),
            P(),
            P(),
            P(),
            P(),
        ),
        out_specs=(P(ROW_COL, None, None), P(ROW_COL, None)),
        check_vma=False,
    )
```

profile of v0, /device:TPU:0, one launch (start us, length us, event | category | flops | bytes accessed | tf_op | source)
XLA Modules:
  0.0 170.9 jit_solution(2306894701090121409)
XLA Ops:
  1.4 0.7 pad_add_fusion
  2.1 0.7 broadcast_in_dim.98
  2.8 11.3 %all-to-all-start = ((s32[128,1,129]{2,1,0:T(1,128)}), s32[128,1,129]{2,1,0:T(1,128)S(1)}, u32[]{:S(2)}, u32[]{:S(2)}) async-start(s32[128,1,129]{2,1,0:T(1,128)} %broadcast_in_dim.98), calls=%async_computation | async-start | bytes 262144 | tf_op jit(solution)/shard_map/all_to_all | solution.py:325
  14.9 8.6 %all-to-all-done = s32[128,1,129]{2,1,0:T(1,128)S(1)} async-done(((s32[128,1,129]{2,1,0:T(1,128)}), s32[128,1,129]{2,1,0:T(1,128)S(1)}, u32[]{:S(2)}, u32[]{:S(2)}) %all-to-all-start) | async-done | bytes 66080 | tf_op jit(solution)/shard_map/all_to_all | solution.py:325
  23.6 0.7 fusion.8.where
  24.3 0.6 copy-done.9
  25.0 8.3 %blend.1 = (bf16[64,112,512]{2,1,0:T(8,128)(2,1)}, bf16[64,16,512]{2,1,0:T(8,128)(2,1)}) custom-call(s32[4]{0:T(128)} %fusion.8.where, f32[1]{0:T(128)S(6)} %copy.32.scale, bf16[64,128,512]{2,1,0:T(8,128)(2,1)} %own.1, bf16[64,128,512]{2,1,0:T(8,128)(2,1)} %collective-permute-done.par, s32[64,2,256]{2,1,0:T(2,128)} %own_edges.1, s32[64,2,256]{2,1,0:T(2,128)} %copy-done.9), custom_call_target="tpu_custom_call" | custom-call | flops 1610612736 | bytes 16777216 | tf_op jit(solution)/shard_map/blend/pallas_call | solution.py:101
  33.3 6.0 %all-to-all-start.1 = ((bf16[64,112,512]{2,1,0:T(8,128)(2,1)}), bf16[64,112,512]{2,1,0:T(8,128)(2,1)}, u32[]{:S(2)}, u32[]{:S(2)}) async-start(bf16[64,112,512]{2,1,0:T(8,128)(2,1)} %get-tuple-element.7.head_ref), calls=%async_computation.1 | async-start | bytes 14680064 | tf_op jit(solution)/shard_map/all_to_all | solution.py:340
  39.6 0.6 fusion.13
  41.5 1.2 compare_select_fusion.1
  42.7 0.6 broadcast_compare_fusion
  43.4 0.7 select_reduce_fusion.3
  44.7 18.6 %pool.1 = f32[64,512]{1,0:T(8,128)} custom-call(s32[64]{0:T(128)} %get-tuple-element.11.counts, bf16[64,112,512]{2,1,0:T(8,128)(2,1)} %get-tuple-element.7.head_ref, bf16[64,16,512]{2,1,0:T(8,128)(2,1)} %get-tuple-element.6.tail_ref, bf16[512,512]{1,0:T(8,128)(2,1)} %refs_0_.5, f32[1,512]{1,0:T(1,128)} %bitcast.24, bf16[512,512]{1,0:T(8,128)(2,1)} %refs_2_.5, ...), custom_call_target="tpu_custom_call" | custom-call | flops 12884901888 | bytes 16777216 | tf_op jit(solution)/shard_map/pool/pallas_call | solution.py:167
  63.3 2.0 %fusion.2 = f32[1024,512]{1,0:T(8,128)S(1)} fusion(f32[64,512]{1,0:T(8,128)} %pool.1, s32[64]{0:T(128)S(1)} %broadcast_select_fusion), kind=kOutput, calls=%fused_computation.7 | convolution fusion | flops 402718720 | bytes 2228480 | tf_op jit(solution)/shard_map/dot_general | solution.py:357
  65.3 0.9 fusion.1
  66.5 1.9 %collective-permute-done.2 = bf16[64,8,512]{2,1,0:T(8,128)(2,1)} collective-permute-done((bf16[64,8,512]{2,1,0:T(8,128)(2,1)}, bf16[64,8,512]{2,1,0:T(8,128)(2,1)}, u32[]{:S(2)}, u32[]{:S(2)}) %collective-permute-start.2) | collective-permute-done | bytes 524320 | tf_op jit(solution)/shard_map/ppermute | solution.py:363
  68.4 1.2 fusion
  69.7 1.3 pad_maximum_fusion
  70.9 62.2 %all-to-all-done.1.arrived = bf16[64,112,512]{2,1,0:T(8,128)(2,1)} async-done(((bf16[64,112,512]{2,1,0:T(8,128)(2,1)}), bf16[64,112,512]{2,1,0:T(8,128)(2,1)}, u32[]{:S(2)}, u32[]{:S(2)}) %all-to-all-start.1) | async-done | bytes 7340064 | tf_op jit(solution)/shard_map/all_to_all | solution.py:340
  133.1 11.0 %all-to-all-start.2 = ((bf16[64,24,512]{2,1,0:T(8,128)(2,1)}), bf16[64,24,512]{2,1,0:T(8,128)(2,1)S(1)}, u32[]{:S(2)}, u32[]{:S(2)}) async-start(bf16[64,24,512]{2,1,0:T(8,128)(2,1)} %pad_maximum_fusion), calls=%async_computation.2 | async-start | bytes 3145728 | tf_op jit(solution)/shard_map/all_to_all | solution.py:366
  144.2 1.6 select_reduce_fusion.counts
  146.4 10.5 %place.1.refs_6_ = bf16[32,128,512]{2,1,0:T(8,128)(2,1)} custom-call(s32[32]{0:T(128)} %broadcast_shift-right-arithmetic_fusion.chips, s32[32]{0:T(128)} %select_reduce_fusion.counts, bf16[64,112,512]{2,1,0:T(8,128)(2,1)} %all-to-all-done.1.arrived, bf16[512,512]{1,0:T(8,128)(2,1)} %refs_0_.5, f32[1,512]{1,0:T(1,128)} %bitcast.25, bf16[512,512]{1,0:T(8,128)(2,1)} %refs_2_.5, ...), custom_call_target="tpu_custom_call" | custom-call | flops 5637144576 | bytes 7340032 | tf_op jit(solution)/shard_map/place/pallas_call | solution.py:227
  157.0 10.7 %all-to-all-done.2.arrived = bf16[64,24,512]{2,1,0:T(8,128)(2,1)S(1)} async-done(((bf16[64,24,512]{2,1,0:T(8,128)(2,1)}), bf16[64,24,512]{2,1,0:T(8,128)(2,1)S(1)}, u32[]{:S(2)}, u32[]{:S(2)}) %all-to-all-start.2) | async-done | bytes 1572896 | tf_op jit(solution)/shard_map/all_to_all | solution.py:366
  167.7 3.2 %finish.1 = (bf16[32,128,512]{2,1,0:T(8,128)(2,1)}, f32[8,512]{1,0:T(8,128)}) custom-call(s32[32]{0:T(128)S(1)} %copy-done.7, s32[32]{0:T(128)S(1)} %copy-done.3, bf16[64,24,512]{2,1,0:T(8,128)(2,1)S(1)} %all-to-all-done.2.arrived, bf16[512,512]{1,0:T(8,128)(2,1)S(1)} %copy-done, f32[1,512]{1,0:T(1,128)S(1)} %bitcast.26, ...), custom_call_target="tpu_custom_call", output_to_operand_aliasing={{0}: (9, {})} | custom-call | flops 805306368 | bytes 1048576 | tf_op jit(solution)/shard_map/finish/pallas_call | solution.py:275
  (46 shorter events, 2.2 us)
Async XLA Ops:
  0.6 23.7 %collective-permute-start = (bf16[64,128,512]{2,1,0:T(8,128)(2,1)}, bf16[64,128,512]{2,1,0:T(8,128)(2,1)}, u32[]{:S(2)}, u32[]{:S(2)}) collective-permute-start(bf16[64,128,512]{2,1,0:T(8,128)(2,1)} %own.1), channel_id=1, source_target_pairs={{0,1},{1,0},{2,3},{3,2},{4,5},{5,4},{6,7},{7,6},{8,9},{9,8},{10,11... | collective-permute-start | bytes 25165832 | tf_op jit(solution)/shard_map/ppermute | solution.py:322
  2.8 20.7 %all-to-all-start = ((s32[128,1,129]{2,1,0:T(1,128)}), s32[128,1,129]{2,1,0:T(1,128)S(1)}, u32[]{:S(2)}, u32[]{:S(2)}) async-start(s32[128,1,129]{2,1,0:T(1,128)} %broadcast_in_dim.98), calls=%async_computation | async-start | bytes 262144 | tf_op jit(solution)/shard_map/all_to_all | solution.py:325
  14.1 10.2 %collective-permute-start.1 = (s32[64,2,256]{2,1,0:T(2,128)}, s32[64,2,256]{2,1,0:T(2,128)S(1)}, u32[]{:S(2)}, u32[]{:S(2)}) collective-permute-start(s32[64,2,256]{2,1,0:T(2,128)} %own_edges.1), channel_id=1, source_target_pairs={{0,1},{1,0},{2,3},{3,2},{4,5},{5,4},{6,7},{7,6},{8,9},{9,8},{10,11... | collective-permute-start | bytes 393224 | tf_op jit(solution)/shard_map/ppermute | solution.py:323
  24.3 0.7 copy-start.9
  33.3 6.3 %copy-start.10 = (s32[4]{0:T(128)S(1)}, s32[4]{0:T(128)}, u32[]{:S(2)}) copy-start(s32[4]{0:T(128)} %fusion.8.where) | copy-start | bytes 52
  33.3 99.8 %all-to-all-start.1 = ((bf16[64,112,512]{2,1,0:T(8,128)(2,1)}), bf16[64,112,512]{2,1,0:T(8,128)(2,1)}, u32[]{:S(2)}, u32[]{:S(2)}) async-start(bf16[64,112,512]{2,1,0:T(8,128)(2,1)} %get-tuple-element.7.head_ref), calls=%async_computation.1 | async-start | bytes 14680064 | tf_op jit(solution)/shard_map/all_to_all | solution.py:340
  63.3 6.4 %copy-start.8 = (bf16[64,16,512]{2,1,0:T(8,128)(2,1)S(1)}, bf16[64,16,512]{2,1,0:T(8,128)(2,1)}, u32[]{:S(2)}) copy-start(bf16[64,16,512]{2,1,0:T(8,128)(2,1)} %get-tuple-element.6.tail_ref) | copy-start | bytes 3145732
  66.2 2.3 %collective-permute-start.2 = (bf16[64,8,512]{2,1,0:T(8,128)(2,1)}, bf16[64,8,512]{2,1,0:T(8,128)(2,1)}, u32[]{:S(2)}, u32[]{:S(2)}) collective-permute-start(bf16[64,8,512]{2,1,0:T(8,128)(2,1)} %fusion.1), channel_id=1, source_target_pairs={{0,1},{1,0},{2,3},{3,2},{4,5},{5,4},{6,7},{7,6},{8,9},{9,8},{10,11... | collective-permute-start | bytes 1572872 | tf_op jit(solution)/shard_map/ppermute | solution.py:363
  133.1 34.6 %all-to-all-start.2 = ((bf16[64,24,512]{2,1,0:T(8,128)(2,1)}), bf16[64,24,512]{2,1,0:T(8,128)(2,1)S(1)}, u32[]{:S(2)}, u32[]{:S(2)}) async-start(bf16[64,24,512]{2,1,0:T(8,128)(2,1)} %pad_maximum_fusion), calls=%async_computation.2 | async-start | bytes 3145728 | tf_op jit(solution)/shard_map/all_to_all | solution.py:366
  146.3 21.3 %copy-start = (bf16[512,512]{1,0:T(8,128)(2,1)S(1)}, bf16[512,512]{1,0:T(8,128)(2,1)}, u32[]{:S(2)}) copy-start(bf16[512,512]{1,0:T(8,128)(2,1)} %refs_0_.5) | copy-start | bytes 1572868
  146.3 21.3 %copy-start.1 = (bf16[512,512]{1,0:T(8,128)(2,1)S(1)}, bf16[512,512]{1,0:T(8,128)(2,1)}, u32[]{:S(2)}) copy-start(bf16[512,512]{1,0:T(8,128)(2,1)} %refs_2_.5) | copy-start | bytes 1572868
  146.3 21.3 %copy-start.2 = (bf16[512,512]{1,0:T(8,128)(2,1)S(1)}, bf16[512,512]{1,0:T(8,128)(2,1)}, u32[]{:S(2)}) copy-start(bf16[512,512]{1,0:T(8,128)(2,1)} %refs_4_.5) | copy-start | bytes 1572868
  146.3 21.3 %copy-start.3 = (s32[32]{0:T(128)S(1)}, s32[32]{0:T(128)}, u32[]{:S(2)}) copy-start(s32[32]{0:T(128)} %select_reduce_fusion.counts) | copy-start | bytes 388
  146.4 21.3 %copy-start.4 = (f32[512]{0:T(512)S(1)}, f32[512]{0:T(512)}, u32[]{:S(2)}) copy-start(f32[512]{0:T(512)} %param.19) | copy-start | bytes 6148
  146.4 21.3 %copy-start.5 = (f32[512]{0:T(512)S(1)}, f32[512]{0:T(512)}, u32[]{:S(2)}) copy-start(f32[512]{0:T(512)} %param.21) | copy-start | bytes 6148
  146.4 21.3 %copy-start.6 = (f32[512]{0:T(512)S(1)}, f32[512]{0:T(512)}, u32[]{:S(2)}) copy-start(f32[512]{0:T(512)} %param.23) | copy-start | bytes 6148
  146.4 21.3 %copy-start.7 = (s32[32]{0:T(128)S(1)}, s32[32]{0:T(128)}, u32[]{:S(2)}) copy-start(s32[32]{0:T(128)} %broadcast_shift-right-arithmetic_fusion.chips) | copy-start | bytes 388
where the time goes:
time: 170 us; the launch traced here: 171 us
  waiting for transfers between devices  83.4 us (49%)
  Pallas kernels  40.7 us (24%)
  starting transfers between devices  28.4 us (17%)
  other arithmetic  9.7 us (6%)
  between operations  3.48 us (2%)
  local copies, waits for them, and re-layouts  3.31 us (2%)
  matrix products  1.97 us (1%)
    all_to_all x1, waiting for transfers between devices, body(): lax.all_to_all(heads, CHIP, split_axis=0, concat_axis=0, tiled=True)  62.2 us
    pallas_call x1, Pallas kernels, pooled_slots(): pl.pallas_call(pool_kernel, out_shape=jax.ShapeDtypeStruct((count, hidden...  18.6 us
    all_to_all x1, starting transfers between devices, body(): lax.all_to_all(jnp.broadcast_to(info[None], (devices, info.shape[0])), RO...  11.3 us
    all_to_all x1, starting transfers between devices, body(): lax.all_to_all(rest, CHIP, split_axis=0, concat_axis=0, tiled=True)  11 us
    all_to_all x1, waiting for transfers between devices, body(): lax.all_to_all(rest, CHIP, split_axis=0, concat_axis=0, tiled=True)  10.7 us
    pallas_call x1, Pallas kernels, placed_heads(): pl.pallas_call(place_kernel, out_shape=jax.ShapeDtypeStruct((G_DEV, nodes...  10.5 us
    all_to_all x1, waiting for transfers between devices, body(): lax.all_to_all(jnp.broadcast_to(info[None], (devices, info.shape[0])), RO...  8.57 us
    pallas_call x1, Pallas kernels, blended_slots(): pl.pallas_call(blend_kernel, out_shape=[jax.ShapeDtypeStruct((count, rows...  8.32 us
  transfers between devices with their start and end apart: 6, of which 4 were waited for; matrix products, arithmetic and copies ran while one was open for 8% of the time, Pallas kernels for 17%

commit v1 on v0

--- a/solution.py
+++ b/solution.py
@@ -14,12 +14,12 @@
 PACK_BITS = 3
 PACK = 1 << PACK_BITS
 POOL = 8
-MLP_BITS = 2
-HEAD_ROWS = 112
-TAIL_GRAPHS = 16
+MLP_BITS = 3
+HEAD_ROWS = 80
+TAIL_BITS = 3
+TAIL_GRAPHS = 1 << TAIL_BITS
 MLP = 1 << MLP_BITS
-VMEM_BYTES = 58 * 1024 * 1024
-FINISH_BYTES = 24 * 1024 * 1024
+VMEM_BYTES = 59 * 1024 * 1024
 
 
 def masked_sum(keep, values, axis):
@@ -242,9 +242,20 @@
 
 
 def finish_kernel(chips, counts, arrived, *refs):
-    weights, (_, out, readout, made, made_sem) = refs[:6], refs[6:]
-    count, tail, hidden = made.shape
+    weights, refs = refs[:6], refs[7:]
+    out, readout, taken, made, terms, taken_sem, made_sem, terms_sem = refs
+    count, tail, hidden = taken.shape
     nodes = out.shape[1]
+    own_rows = pl.ds(0, tail)
+
+    @pl.loop(0, count)
+    def _(slot):
+        pltpu.make_async_copy(
+            arrived.at[chips[slot], own_rows], taken.at[slot], taken_sem.at[slot >> TAIL_BITS]
+        ).start()
+
+    summed = pltpu.make_async_copy(arrived.at[:, pl.ds(tail, READ_DEV)], terms, terms_sem)
+    summed.start()
 
     def put(group):
         rows = pl.ds(group * TAIL_GRAPHS, TAIL_GRAPHS)
@@ -253,16 +264,25 @@
         )
 
     node_index = nodes - tail + lax.broadcasted_iota(jnp.int32, (tail, 1), 0)
-    for group in range(count // TAIL_GRAPHS):
-        slots = [group * TAIL_GRAPHS + lane for lane in range(TAIL_GRAPHS)]
-        rows = jnp.concatenate([arrived[chips[slot], :tail] for slot in slots], axis=0)
-        result = perceptron(rows, weights)
-        for lane, slot in enumerate(slots):
+
+    @pl.loop(0, count // TAIL_GRAPHS)
+    def _(group):
+        rows = pl.ds(group * TAIL_GRAPHS, TAIL_GRAPHS)
+        pltpu.make_async_copy(
+            arrived.at[pl.ds(0, TAIL_GRAPHS), own_rows], taken.at[rows], taken_sem.at[group]
+        ).wait()
+        result = perceptron(taken[rows].reshape(TAIL_GRAPHS * tail, hidden), weights)
+        for lane in range(TAIL_GRAPHS):
+            slot = group * TAIL_GRAPHS + lane
             part = result[lane * tail : (lane + 1) * tail]
             made[slot] = jnp.where(node_index < counts[slot], part, 0.0).astype(jnp.bfloat16)
         put(group).start()
-    readout[...] = jnp.sum(arrived[:, tail:].astype(jnp.float32), axis=0)
-    for group in range(count // TAIL_GRAPHS):
+
+    summed.wait()
+    readout[...] = jnp.sum(terms[...].astype(jnp.float32), axis=0)
+
+    @pl.loop(0, count // TAIL_GRAPHS)
+    def _(group):
         put(group).wait()
 
 
@@ -278,14 +298,18 @@
             jax.ShapeDtypeStruct(node_out.shape, jnp.bfloat16),
             jax.ShapeDtypeStruct((READ_DEV, hidden), jnp.float32),
         ],
-        in_specs=[scalar, scalar, vector] + [vector] * 6 + [anywhere],
+        in_specs=[scalar, scalar, anywhere] + [vector] * 6 + [anywhere],
         out_specs=[anywhere, vector],
         scratch_shapes=[
             pltpu.VMEM((count, tail, hidden), jnp.bfloat16),
+            pltpu.VMEM((count, tail, hidden), jnp.bfloat16),
+            pltpu.VMEM((arrived.shape[0], READ_DEV, hidden), jnp.bfloat16),
             pltpu.SemaphoreType.DMA((count // TAIL_GRAPHS,)),
+            pltpu.SemaphoreType.DMA((count // TAIL_GRAPHS,)),
+            pltpu.SemaphoreType.DMA,
         ],
         input_output_aliases={9: 0},
-        compiler_params=pltpu.CompilerParams(vmem_limit_bytes=FINISH_BYTES),
+        compiler_params=pltpu.CompilerParams(vmem_limit_bytes=VMEM_BYTES),
         cost_estimate=mlp_cost(count * tail, hidden),
         name="finish",
     )(chips, counts, arrived, *weights, node_out)

time: 170 us -> 172 us (1.012); the launches traced: 171 us -> 170 us
  starting transfers between devices: 28.4 us -> 25.9 us
  Pallas kernels: 40.7 us -> 42.5 us
    all_to_all x1, waiting for transfers between devices: 62.2 us -> 34.7 us  [body(): lax.all_to_all(heads, CHIP, split_axis=0, concat_axis=0, tiled=True)]
    all_to_all x1, waiting for transfers between devices: 10.7 us -> 37.5 us  [body(): lax.all_to_all(rest, CHIP, split_axis=0, concat_axis=0, tiled=True)]
    pallas_call x1, Pallas kernels: 3.18 us -> 7.35 us  [finished(): pl.pallas_call(finish_kernel, out_shape=[jax.ShapeDtypeStruct(node_out.sh...]
    concatenate x1, other arithmetic: 1.27 us -> 3.97 us  [body(): rest = jnp.concatenate([tails, both.astype(jnp.bfloat16)], axis=1)]
    all_to_all x1, starting transfers between devices: 11 us -> 8.5 us  [body(): lax.all_to_all(rest, CHIP, split_axis=0, concat_axis=0, tiled=True)]
    pallas_call x1, Pallas kernels: 10.5 us -> 8.24 us  [placed_heads(): pl.pallas_call(place_kernel, out_shape=jax.ShapeDtypeStruct((G_DEV, nodes...]
  transfers between devices with their start and end apart: 6 -> 6, of which waited for: 4 -> 4; matrix products, arithmetic and copies ran while one was open for 8% -> 9% of each run, Pallas kernels for 17% -> 16%
where the time goes in v1:
time: 172 us; the launch traced here: 170 us
  waiting for transfers between devices  82.7 us (48%)
  Pallas kernels  42.5 us (25%)
  starting transfers between devices  25.9 us (15%)
  other arithmetic  11.4 us (7%)
  between operations  3.45 us (2%)
  local copies, waits for them, and re-layouts  2.47 us (1%)
  matrix products  1.88 us (1%)
    all_to_all x1, waiting for transfers between devices, body(): lax.all_to_all(rest, CHIP, split_axis=0, concat_axis=0, tiled=True)  37.5 us
    all_to_all x1, waiting for transfers between devices, body(): lax.all_to_all(heads, CHIP, split_axis=0, concat_axis=0, tiled=True)  34.7 us
    pallas_call x1, Pallas kernels, pooled_slots(): pl.pallas_call(pool_kernel, out_shape=jax.ShapeDtypeStruct((count, hidden...  18.6 us
    all_to_all x1, starting transfers between devices, body(): lax.all_to_all(jnp.broadcast_to(info[None], (devices, info.shape[0])), RO...  11.3 us
    all_to_all x1, waiting for transfers between devices, body(): lax.all_to_all(jnp.broadcast_to(info[None], (devices, info.shape[0])), RO...  8.57 us
    all_to_all x1, starting transfers between devices, body(): lax.all_to_all(rest, CHIP, split_axis=0, concat_axis=0, tiled=True)  8.5 us
    pallas_call x1, Pallas kernels, blended_slots(): pl.pallas_call(blend_kernel, out_shape=[jax.ShapeDtypeStruct((count, rows...  8.32 us
    pallas_call x1, Pallas kernels, placed_heads(): pl.pallas_call(place_kernel, out_shape=jax.ShapeDtypeStruct((G_DEV, nodes...  8.24 us
  transfers between devices with their start and end apart: 6, of which 4 were waited for; matrix products, arithmetic and copies ran while one was open for 9% of the time, Pallas kernels for 16%

profile of v1, /device:TPU:0, one launch (start us, length us, event | category | flops | bytes accessed | tf_op | source)
XLA Modules:
  0.0 170.4 jit_solution(74886043434271386)
XLA Ops:
  1.4 0.7 pad_add_fusion
  2.1 0.7 broadcast_in_dim.98
  2.8 11.3 %all-to-all-start = ((s32[128,1,129]{2,1,0:T(1,128)}), s32[128,1,129]{2,1,0:T(1,128)S(1)}, u32[]{:S(2)}, u32[]{:S(2)}) async-start(s32[128,1,129]{2,1,0:T(1,128)} %broadcast_in_dim.98), calls=%async_computation | async-start | bytes 262144 | tf_op jit(solution)/shard_map/all_to_all | solution.py:349
  14.9 8.6 %all-to-all-done = s32[128,1,129]{2,1,0:T(1,128)S(1)} async-done(((s32[128,1,129]{2,1,0:T(1,128)}), s32[128,1,129]{2,1,0:T(1,128)S(1)}, u32[]{:S(2)}, u32[]{:S(2)}) %all-to-all-start) | async-done | bytes 66080 | tf_op jit(solution)/shard_map/all_to_all | solution.py:349
  23.6 0.7 fusion.8.where
  24.3 0.6 copy-done
  25.0 8.3 %blend.1 = (bf16[64,80,512]{2,1,0:T(8,128)(2,1)}, bf16[64,48,512]{2,1,0:T(8,128)(2,1)}) custom-call(s32[4]{0:T(128)} %fusion.8.where, f32[1]{0:T(128)S(6)} %copy.32.scale, bf16[64,128,512]{2,1,0:T(8,128)(2,1)} %own.1, bf16[64,128,512]{2,1,0:T(8,128)(2,1)} %collective-permute-done.par, s32[64,2,256]{2,1,0:T(2,128)} %own_edges.1, s32[64,2,256]{2,1,0:T(2,128)} %copy-done), custom_call_target="tpu_custom_call" | custom-call | flops 1610612736 | bytes 16777216 | tf_op jit(solution)/shard_map/blend/pallas_call | solution.py:101
  33.3 5.9 %all-to-all-start.1 = ((bf16[64,80,512]{2,1,0:T(8,128)(2,1)}), bf16[64,80,512]{2,1,0:T(8,128)(2,1)}, u32[]{:S(2)}, u32[]{:S(2)}) async-start(bf16[64,80,512]{2,1,0:T(8,128)(2,1)} %get-tuple-element.7.head_ref), calls=%async_computation.1 | async-start | bytes 10485760 | tf_op jit(solution)/shard_map/all_to_all | solution.py:364
  39.5 0.7 fusion.13
  41.4 1.3 compare_select_fusion.1
  42.7 0.6 broadcast_compare_fusion
  43.3 0.7 select_reduce_fusion.3
  44.0 0.6 broadcast_select_fusion
  44.7 18.6 %pool.1 = f32[64,512]{1,0:T(8,128)} custom-call(s32[64]{0:T(128)} %get-tuple-element.11.counts, bf16[64,80,512]{2,1,0:T(8,128)(2,1)} %get-tuple-element.7.head_ref, bf16[64,48,512]{2,1,0:T(8,128)(2,1)} %get-tuple-element.6.tail_ref, bf16[512,512]{1,0:T(8,128)(2,1)} %refs_0_.5, f32[1,512]{1,0:T(1,128)} %bitcast.29, bf16[512,512]{1,0:T(8,128)(2,1)} %refs_2_.5, ...), custom_call_target="tpu_custom_call" | custom-call | flops 12884901888 | bytes 16777216 | tf_op jit(solution)/shard_map/pool/pallas_call | solution.py:167
  63.3 1.9 %fusion.2 = f32[1024,512]{1,0:T(8,128)S(1)} fusion(f32[64,512]{1,0:T(8,128)} %pool.1, s32[64]{0:T(128)S(1)} %broadcast_select_fusion), kind=kOutput, calls=%fused_computation.7 | convolution fusion | flops 402718720 | bytes 2228480 | tf_op jit(solution)/shard_map/dot_general | solution.py:381
  65.4 1.9 %collective-permute-done.2 = bf16[64,8,512]{2,1,0:T(8,128)(2,1)S(1)} collective-permute-done((bf16[64,8,512]{2,1,0:T(8,128)(2,1)S(1)}, bf16[64,8,512]{2,1,0:T(8,128)(2,1)S(1)}, u32[]{:S(2)}, u32[]{:S(2)}) %collective-permute-start.2) | collective-permute-done | bytes 524320 | tf_op jit(solution)/shard_map/ppermute | solution.py:387
  67.4 4.0 %pad_maximum_fusion = bf16[64,56,512]{2,1,0:T(8,128)(2,1)} fusion(bf16[64,8,512]{2,1,0:T(8,128)(2,1)S(1)} %fusion, bf16[64,48,512]{2,1,0:T(8,128)(2,1)} %get-tuple-element.6.tail_ref), kind=kLoop, calls=%fused_computation | loop fusion | flops 7340032 | bytes 7340032 | tf_op jit(solution)/shard_map/concatenate | solution.py:388
  71.4 34.7 %all-to-all-done.1.arrived = bf16[64,80,512]{2,1,0:T(8,128)(2,1)} async-done(((bf16[64,80,512]{2,1,0:T(8,128)(2,1)}), bf16[64,80,512]{2,1,0:T(8,128)(2,1)}, u32[]{:S(2)}, u32[]{:S(2)}) %all-to-all-start.1) | async-done | bytes 5242912 | tf_op jit(solution)/shard_map/all_to_all | solution.py:364
  106.1 8.5 %all-to-all-start.2 = ((bf16[64,56,512]{2,1,0:T(8,128)(2,1)}), bf16[64,56,512]{2,1,0:T(8,128)(2,1)}, u32[]{:S(2)}, u32[]{:S(2)}) async-start(bf16[64,56,512]{2,1,0:T(8,128)(2,1)} %pad_maximum_fusion), calls=%async_computation.2 | async-start | bytes 7340032 | tf_op jit(solution)/shard_map/all_to_all | solution.py:390
  115.1 1.6 select_reduce_fusion.counts
  116.7 0.5 broadcast_shift-right-arithmetic_fusion.chips
  117.2 8.2 %place.1.refs_6_ = bf16[32,128,512]{2,1,0:T(8,128)(2,1)} custom-call(s32[32]{0:T(128)} %broadcast_shift-right-arithmetic_fusion.chips, s32[32]{0:T(128)} %select_reduce_fusion.counts, bf16[64,80,512]{2,1,0:T(8,128)(2,1)} %all-to-all-done.1.arrived, bf16[512,512]{1,0:T(8,128)(2,1)} %refs_0_.5, f32[1,512]{1,0:T(1,128)} %bitcast.30, bf16[512,512]{1,0:T(8,128)(2,1)} %refs_2_.5, ...), custom_call_target="tpu_custom_call" | custom-call | flops 4026531840 | bytes 5242880 | tf_op jit(solution)/shard_map/place/pallas_call | solution.py:227
  125.5 37.5 %all-to-all-done.2.arrived = bf16[64,56,512]{2,1,0:T(8,128)(2,1)} async-done(((bf16[64,56,512]{2,1,0:T(8,128)(2,1)}), bf16[64,56,512]{2,1,0:T(8,128)(2,1)}, u32[]{:S(2)}, u32[]{:S(2)}) %all-to-all-start.2) | async-done | bytes 3670048 | tf_op jit(solution)/shard_map/all_to_all | solution.py:390
  163.0 7.4 %finish.1 = (bf16[32,128,512]{2,1,0:T(8,128)(2,1)}, f32[8,512]{1,0:T(8,128)}) custom-call(s32[32]{0:T(128)} %broadcast_shift-right-arithmetic_fusion.chips, s32[32]{0:T(128)} %select_reduce_fusion.counts, bf16[64,56,512]{2,1,0:T(8,128)(2,1)} %all-to-all-done.2.arrived, bf16[512,512]{1,0:T(8,128)(2,1)} %refs_0_.5, ...), custom_call_target="tpu_custom_call", output_to_operand_aliasing={{0}: (9, {})} | custom-call | flops 2415919104 | bytes 3145728 | tf_op jit(solution)/shard_map/finish/pallas_call | solution.py:295
  (28 shorter events, 1.3 us)
Async XLA Ops:
  0.6 23.7 %collective-permute-start = (bf16[64,128,512]{2,1,0:T(8,128)(2,1)}, bf16[64,128,512]{2,1,0:T(8,128)(2,1)}, u32[]{:S(2)}, u32[]{:S(2)}) collective-permute-start(bf16[64,128,512]{2,1,0:T(8,128)(2,1)} %own.1), channel_id=1, source_target_pairs={{0,1},{1,0},{2,3},{3,2},{4,5},{5,4},{6,7},{7,6},{8,9},{9,8},{10,11... | collective-permute-start | bytes 25165832 | tf_op jit(solution)/shard_map/ppermute | solution.py:346
  2.8 20.7 %all-to-all-start = ((s32[128,1,129]{2,1,0:T(1,128)}), s32[128,1,129]{2,1,0:T(1,128)S(1)}, u32[]{:S(2)}, u32[]{:S(2)}) async-start(s32[128,1,129]{2,1,0:T(1,128)} %broadcast_in_dim.98), calls=%async_computation | async-start | bytes 262144 | tf_op jit(solution)/shard_map/all_to_all | solution.py:349
  14.1 10.2 %collective-permute-start.1 = (s32[64,2,256]{2,1,0:T(2,128)}, s32[64,2,256]{2,1,0:T(2,128)S(1)}, u32[]{:S(2)}, u32[]{:S(2)}) collective-permute-start(s32[64,2,256]{2,1,0:T(2,128)} %own_edges.1), channel_id=1, source_target_pairs={{0,1},{1,0},{2,3},{3,2},{4,5},{5,4},{6,7},{7,6},{8,9},{9,8},{10,11... | collective-permute-start | bytes 393224 | tf_op jit(solution)/shard_map/ppermute | solution.py:347
  24.3 0.7 copy-start
  33.3 6.2 %copy-start.1 = (s32[4]{0:T(128)S(1)}, s32[4]{0:T(128)}, u32[]{:S(2)}) copy-start(s32[4]{0:T(128)} %fusion.8.where) | copy-start | bytes 52
  33.3 72.8 %all-to-all-start.1 = ((bf16[64,80,512]{2,1,0:T(8,128)(2,1)}), bf16[64,80,512]{2,1,0:T(8,128)(2,1)}, u32[]{:S(2)}, u32[]{:S(2)}) async-start(bf16[64,80,512]{2,1,0:T(8,128)(2,1)} %get-tuple-element.7.head_ref), calls=%async_computation.1 | async-start | bytes 10485760 | tf_op jit(solution)/shard_map/all_to_all | solution.py:364
  65.3 2.0 %collective-permute-start.2 = (bf16[64,8,512]{2,1,0:T(8,128)(2,1)S(1)}, bf16[64,8,512]{2,1,0:T(8,128)(2,1)S(1)}, u32[]{:S(2)}, u32[]{:S(2)}) collective-permute-start(bf16[64,8,512]{2,1,0:T(8,128)(2,1)S(1)} %fusion.1), channel_id=1, source_target_pairs={{0,1},{1,0},{2,3},{3,2},{4,5},{5,4},{6,7},{7,6},{8,9},{9,8},{10,11... | collective-permute-start | bytes 1572872 | tf_op jit(solution)/shard_map/ppermute | solution.py:387
  106.1 56.9 %all-to-all-start.2 = ((bf16[64,56,512]{2,1,0:T(8,128)(2,1)}), bf16[64,56,512]{2,1,0:T(8,128)(2,1)}, u32[]{:S(2)}, u32[]{:S(2)}) async-start(bf16[64,56,512]{2,1,0:T(8,128)(2,1)} %pad_maximum_fusion), calls=%async_computation.2 | async-start | bytes 7340032 | tf_op jit(solution)/shard_map/all_to_all | solution.py:390

commit v2 on v1

--- a/solution.py
+++ b/solution.py
@@ -1,3 +1,5 @@
+import functools
+
 import jax
 import jax.numpy as jnp
 from jax import lax
@@ -20,6 +22,7 @@
 TAIL_GRAPHS = 1 << TAIL_BITS
 MLP = 1 << MLP_BITS
 VMEM_BYTES = 59 * 1024 * 1024
+BLEND_BYTES = 56 * 1024 * 1024
 
 
 def masked_sum(keep, values, axis):
@@ -27,12 +30,14 @@
 
 
 def blend_kernel(
-    where, scale, own, par, own_edges, par_edges, head, tail, taken, made, taken_sem, made_sem
+    first, where, scale, own, par, own_edges, par_edges, out, taken, made, taken_sem, made_sem
 ):
     core, offset, live_a, live_b = where[0], where[1], where[2], where[3]
     count, nodes, _ = taken.shape
+    size = made.shape[1]
     wrap = 2 * count - 1
     node_index = lax.broadcasted_iota(jnp.int32, (nodes, own_edges.shape[-1]), 0)
+    row_index = first + lax.broadcasted_iota(jnp.int32, (size, own_edges.shape[-1]), 0)
 
     def source_of(slot):
         number = (2 * slot + core - offset) & wrap
@@ -54,12 +59,9 @@
         def _():
             pltpu.make_async_copy(own.at[index], taken.at[slot], sem).start()
 
-    cuts = ((head, pl.ds(0, HEAD_ROWS)), (tail, pl.ds(HEAD_ROWS, nodes - HEAD_ROWS)))
-
-    def put(group, which):
+    def put(group):
         rows = pl.ds(group * PACK, PACK)
-        out, cut = cuts[which]
-        return pltpu.make_async_copy(made.at[rows, cut], out.at[rows], made_sem.at[which, group])
+        return pltpu.make_async_copy(made.at[rows], out.at[rows], made_sem.at[group])
 
     @pl.loop(0, count // PACK)
     def _(group):
@@ -72,7 +74,7 @@
             index, from_par = source_of(slot)
             edges = jnp.where(from_par, par_edges[index], own_edges[index])
             sources.append((node_index == edges[0:1, :]).astype(jnp.bfloat16))
-            targets.append((node_index == edges[1:2, :]).astype(jnp.bfloat16))
+            targets.append((row_index == edges[1:2, :]).astype(jnp.bfloat16))
         adjacency = [
             lax.dot_general(t, s, (((1,), (1,)), ((), ())), preferred_element_type=jnp.float32)
             for t, s in zip(targets, sources)
@@ -83,38 +85,34 @@
             for a, f in zip(adjacency, features)
         ]
         for slot, f, n in zip(slots, features, neighbours):
-            made[slot] = (scale[0] * f.astype(jnp.float32) + n).astype(jnp.bfloat16)
-        put(group, 0).start()
-        put(group, 1).start()
+            kept = f[first : first + size].astype(jnp.float32)
+            made[slot] = (scale[0] * kept + n).astype(jnp.bfloat16)
+        put(group).start()
 
     @pl.loop(0, count // PACK)
     def _(group):
-        put(group, 0).wait()
-        put(group, 1).wait()
-
-
-def blended_slots(own, par, own_edges, par_edges, where, scale):
+        put(group).wait()
+
+
+def blended_slots(own, par, own_edges, par_edges, where, scale, first, size):
     count, nodes, hidden = own.shape
     anywhere = pl.BlockSpec(memory_space=pl.ANY)
     vector = pl.BlockSpec(memory_space=pltpu.VMEM)
     scalar = pl.BlockSpec(memory_space=pltpu.SMEM)
     return pl.pallas_call(
-        blend_kernel,
-        out_shape=[
-            jax.ShapeDtypeStruct((count, rows, hidden), jnp.bfloat16)
-            for rows in (HEAD_ROWS, nodes - HEAD_ROWS)
-        ],
+        functools.partial(blend_kernel, first),
+        out_shape=jax.ShapeDtypeStruct((count, size, hidden), jnp.bfloat16),
         in_specs=[scalar, scalar, anywhere, anywhere, vector, vector],
-        out_specs=[anywhere, anywhere],
+        out_specs=anywhere,
         scratch_shapes=[
             pltpu.VMEM((count, nodes, hidden), jnp.bfloat16),
-            pltpu.VMEM((count, nodes, hidden), jnp.bfloat16),
+            pltpu.VMEM((count, size, hidden), jnp.bfloat16),
             pltpu.SemaphoreType.DMA((count // PACK,)),
-            pltpu.SemaphoreType.DMA((2, count // PACK)),
+            pltpu.SemaphoreType.DMA((count // PACK,)),
         ],
-        compiler_params=pltpu.CompilerParams(vmem_limit_bytes=VMEM_BYTES),
+        compiler_params=pltpu.CompilerParams(vmem_limit_bytes=BLEND_BYTES),
         cost_estimate=pl.CostEstimate(
-            flops=2 * count * nodes * nodes * (own_edges.shape[-1] + hidden),
+            flops=2 * count * size * nodes * (own_edges.shape[-1] + hidden),
             bytes_accessed=4 * count * nodes * hidden,
             transcendentals=0,
         ),
@@ -358,10 +356,10 @@
     own = (part == 0) & (device < core)
     place = masked_sum(ahead | mine | own, jnp.where(own, 1, live[None, :]), 1)
 
-    heads, tails = blended_slots(
-        node_features, par_features, edge_list, par_edges, place, self_weight
-    )
+    graphs = (node_features, par_features, edge_list, par_edges, place, self_weight)
+    heads = blended_slots(*graphs, 0, HEAD_ROWS)
     arrived = lax.all_to_all(heads, CHIP, split_axis=0, concat_axis=0, tiled=True)
+    tails = blended_slots(*graphs, HEAD_ROWS, nodes - HEAD_ROWS)
 
     offset, live_a, live_b = place[1], place[2], place[3]
     slot = lax.broadcasted_iota(jnp.int32, (devices // 2,), 0)

time: 172 us -> 170 us (0.988)
  waiting for transfers between devices: 82.7 us -> 74.3 us
  Pallas kernels: 42.5 us -> 48.4 us
  local copies, waits for them, and re-layouts: 2.47 us -> 4.61 us
    all_to_all x1, waiting for transfers between devices: 34.7 us -> 26 us  [body(): lax.all_to_all(heads, CHIP, split_axis=0, concat_axis=0, tiled=True)]
    pallas_call x1 -> x2, Pallas kernels: 8.32 us -> 14.2 us  [blended_slots(): pl.pallas_call(functools.partial(blend_kernel, first), out_shape=jax.Shap...]
    concatenate x1, other arithmetic: 3.97 us -> 2.09 us  [body(): rest = jnp.concatenate([tails, both.astype(jnp.bfloat16)], axis=1)]
  transfers between devices with their start and end apart: 6 -> 6, of which waited for: 4 -> 4; matrix products, arithmetic and copies ran while one was open for 9% -> 9% of each run, Pallas kernels for 16% -> 20%
where the time goes in v2:
time: 170 us; the launch traced here: 169 us
  waiting for transfers between devices  74.3 us (44%)
  Pallas kernels  48.4 us (28%)
  starting transfers between devices  25.4 us (15%)
  other arithmetic  11 us (6%)
  local copies, waits for them, and re-layouts  4.61 us (3%)
  between operations  3.49 us (2%)
  matrix products  2.03 us (1%)
    all_to_all x1, waiting for transfers between devices, body(): lax.all_to_all(rest, CHIP, split_axis=0, concat_axis=0, tiled=True)  37.5 us
    all_to_all x1, waiting for transfers between devices, body(): lax.all_to_all(heads, CHIP, split_axis=0, concat_axis=0, tiled=True)  26 us
    pallas_call x1, Pallas kernels, pooled_slots(): pl.pallas_call(pool_kernel, out_shape=jax.ShapeDtypeStruct((count, hidden...  18.6 us
    pallas_call x2, Pallas kernels, blended_slots(): pl.pallas_call(functools.partial(blend_kernel, first), out_shape=jax.Shap...  14.2 us
    all_to_all x1, starting transfers between devices, body(): lax.all_to_all(jnp.broadcast_to(info[None], (devices, info.shape[0])), RO...  11.3 us
    all_to_all x1, waiting for transfers between devices, body(): lax.all_to_all(jnp.broadcast_to(info[None], (devices, info.shape[0])), RO...  8.57 us
    pallas_call x1, Pallas kernels, placed_heads(): pl.pallas_call(place_kernel, out_shape=jax.ShapeDtypeStruct((G_DEV, nodes...  8.24 us
    all_to_all x1, starting transfers between devices, body(): lax.all_to_all(rest, CHIP, split_axis=0, concat_axis=0, tiled=True)  8.14 us
  transfers between devices with their start and end apart: 6, of which 4 were waited for; matrix products, arithmetic and copies ran while one was open for 9% of the time, Pallas kernels for 20%

profile of v2, /device:TPU:0, one launch (start us, length us, event | category | flops | bytes accessed | tf_op | source)
XLA Modules:
  0.0 169.3 jit_solution(14847990276965622382)
XLA Ops:
  1.4 0.7 pad_add_fusion
  2.1 0.7 broadcast_in_dim.98
  2.8 11.3 %all-to-all-start = ((s32[128,1,129]{2,1,0:T(1,128)}), s32[128,1,129]{2,1,0:T(1,128)S(1)}, u32[]{:S(2)}, u32[]{:S(2)}) async-start(s32[128,1,129]{2,1,0:T(1,128)} %broadcast_in_dim.98), calls=%async_computation | async-start | bytes 262144 | tf_op jit(solution)/shard_map/all_to_all | solution.py:347
  14.9 8.6 %all-to-all-done = s32[128,1,129]{2,1,0:T(1,128)S(1)} async-done(((s32[128,1,129]{2,1,0:T(1,128)}), s32[128,1,129]{2,1,0:T(1,128)S(1)}, u32[]{:S(2)}, u32[]{:S(2)}) %all-to-all-start) | async-done | bytes 66080 | tf_op jit(solution)/shard_map/all_to_all | solution.py:347
  23.6 0.7 fusion.8.where
  25.0 7.3 %blend.3.head_ref = bf16[64,80,512]{2,1,0:T(8,128)(2,1)} custom-call(s32[4]{0:T(128)} %fusion.8.where, f32[1]{0:T(128)S(6)} %copy.32.scale, bf16[64,128,512]{2,1,0:T(8,128)(2,1)} %own.3, bf16[64,128,512]{2,1,0:T(8,128)(2,1)} %collective-permute-done.par, s32[64,2,256]{2,1,0:T(2,128)} %own_edges.3, s32[64,2,256]{2,1,0:T(2,128)} %copy-done.2), custom_call_target="tpu_custom_call" | custom-call | flops 1006632960 | bytes 16777216 | tf_op jit(solution)/shard_map/blend/pallas_call | solution.py:102
  32.3 5.8 %all-to-all-start.1 = ((bf16[64,80,512]{2,1,0:T(8,128)(2,1)}), bf16[64,80,512]{2,1,0:T(8,128)(2,1)}, u32[]{:S(2)}, u32[]{:S(2)}) async-start(bf16[64,80,512]{2,1,0:T(8,128)(2,1)} %blend.3.head_ref), calls=%async_computation.1 | async-start | bytes 10485760 | tf_op jit(solution)/shard_map/all_to_all | solution.py:361
  38.3 0.6 fusion.13
  40.3 1.3 compare_select_fusion.1
  42.3 0.8 select_reduce_fusion.3
  43.7 6.9 %blend.2.tail_ref = bf16[64,48,512]{2,1,0:T(8,128)(2,1)} custom-call(s32[4]{0:T(128)} %fusion.8.where, f32[1]{0:T(128)S(6)} %copy.32.scale, bf16[64,128,512]{2,1,0:T(8,128)(2,1)} %own.3, bf16[64,128,512]{2,1,0:T(8,128)(2,1)} %collective-permute-done.par, s32[64,2,256]{2,1,0:T(2,128)} %own_edges.3, s32[64,2,256]{2,1,0:T(2,128)} %copy-done.2), custom_call_target="tpu_custom_call" | custom-call | flops 603979776 | bytes 16777216 | tf_op jit(solution)/shard_map/blend/pallas_call | solution.py:102
  50.6 18.6 %pool.1 = f32[64,512]{1,0:T(8,128)} custom-call(s32[64]{0:T(128)} %get-tuple-element.7.counts, bf16[64,80,512]{2,1,0:T(8,128)(2,1)} %blend.3.head_ref, bf16[64,48,512]{2,1,0:T(8,128)(2,1)} %blend.2.tail_ref, bf16[512,512]{1,0:T(8,128)(2,1)} %refs_0_.5, f32[1,512]{1,0:T(1,128)} %bitcast.29, bf16[512,512]{1,0:T(8,128)(2,1)} %refs_2_.5, f32[1,512]{1,0:T(1,128)} %bitcast.32, ...), custom_call_target="tpu_custom_call" | custom-call | flops 12884901888 | bytes 16777216 | tf_op jit(solution)/shard_map/pool/pallas_call | solution.py:165
  69.2 2.0 %fusion.2 = f32[1024,512]{1,0:T(8,128)S(1)} fusion(f32[64,512]{1,0:T(8,128)} %pool.1, s32[64]{0:T(128)S(1)} %broadcast_select_fusion), kind=kOutput, calls=%fused_computation.7 | convolution fusion | flops 402718720 | bytes 2228480 | tf_op jit(solution)/shard_map/dot_general | solution.py:379
  71.3 1.3 copy-done.1
  72.6 0.9 fusion.1
  73.5 2.2 %collective-permute-done.2 = bf16[64,8,512]{2,1,0:T(8,128)(2,1)} collective-permute-done((bf16[64,8,512]{2,1,0:T(8,128)(2,1)}, bf16[64,8,512]{2,1,0:T(8,128)(2,1)}, u32[]{:S(2)}, u32[]{:S(2)}) %collective-permute-start.2) | collective-permute-done | bytes 524320 | tf_op jit(solution)/shard_map/ppermute | solution.py:385
  75.8 1.6 fusion
  77.3 2.1 %pad_maximum_fusion = bf16[64,56,512]{2,1,0:T(8,128)(2,1)} fusion(bf16[64,8,512]{2,1,0:T(8,128)(2,1)S(1)} %fusion, bf16[64,48,512]{2,1,0:T(8,128)(2,1)S(1)} %copy-done), kind=kLoop, calls=%fused_computation | loop fusion | flops 7340032 | bytes 7340032 | tf_op jit(solution)/shard_map/concatenate | solution.py:386
  79.4 26.0 %all-to-all-done.1.arrived = bf16[64,80,512]{2,1,0:T(8,128)(2,1)} async-done(((bf16[64,80,512]{2,1,0:T(8,128)(2,1)}), bf16[64,80,512]{2,1,0:T(8,128)(2,1)}, u32[]{:S(2)}, u32[]{:S(2)}) %all-to-all-start.1) | async-done | bytes 5242912 | tf_op jit(solution)/shard_map/all_to_all | solution.py:361
  105.4 8.1 %all-to-all-start.2 = ((bf16[64,56,512]{2,1,0:T(8,128)(2,1)}), bf16[64,56,512]{2,1,0:T(8,128)(2,1)}, u32[]{:S(2)}, u32[]{:S(2)}) async-start(bf16[64,56,512]{2,1,0:T(8,128)(2,1)} %pad_maximum_fusion), calls=%async_computation.2 | async-start | bytes 7340032 | tf_op jit(solution)/shard_map/all_to_all | solution.py:388
  114.1 1.5 select_reduce_fusion.counts
  116.2 8.2 %place.1.refs_6_ = bf16[32,128,512]{2,1,0:T(8,128)(2,1)} custom-call(s32[32]{0:T(128)} %broadcast_shift-right-arithmetic_fusion.chips, s32[32]{0:T(128)} %select_reduce_fusion.counts, bf16[64,80,512]{2,1,0:T(8,128)(2,1)} %all-to-all-done.1.arrived, bf16[512,512]{1,0:T(8,128)(2,1)} %refs_0_.5, f32[1,512]{1,0:T(1,128)} %bitcast.30, bf16[512,512]{1,0:T(8,128)(2,1)} %refs_2_.5, ...), custom_call_target="tpu_custom_call" | custom-call | flops 4026531840 | bytes 5242880 | tf_op jit(solution)/shard_map/place/pallas_call | solution.py:225
  124.4 37.5 %all-to-all-done.2.arrived = bf16[64,56,512]{2,1,0:T(8,128)(2,1)} async-done(((bf16[64,56,512]{2,1,0:T(8,128)(2,1)}), bf16[64,56,512]{2,1,0:T(8,128)(2,1)}, u32[]{:S(2)}, u32[]{:S(2)}) %all-to-all-start.2) | async-done | bytes 3670048 | tf_op jit(solution)/shard_map/all_to_all | solution.py:388
  161.9 7.3 %finish.1 = (bf16[32,128,512]{2,1,0:T(8,128)(2,1)}, f32[8,512]{1,0:T(8,128)}) custom-call(s32[32]{0:T(128)} %broadcast_shift-right-arithmetic_fusion.chips, s32[32]{0:T(128)} %select_reduce_fusion.counts, bf16[64,56,512]{2,1,0:T(8,128)(2,1)} %all-to-all-done.2.arrived, bf16[512,512]{1,0:T(8,128)(2,1)} %refs_0_.5, ...), custom_call_target="tpu_custom_call", output_to_operand_aliasing={{0}: (9, {})} | custom-call | flops 2415919104 | bytes 3145728 | tf_op jit(solution)/shard_map/finish/pallas_call | solution.py:293
  (33 shorter events, 3.5 us)
Async XLA Ops:
  0.6 23.7 %collective-permute-start = (bf16[64,128,512]{2,1,0:T(8,128)(2,1)}, bf16[64,128,512]{2,1,0:T(8,128)(2,1)}, u32[]{:S(2)}, u32[]{:S(2)}) collective-permute-start(bf16[64,128,512]{2,1,0:T(8,128)(2,1)} %own.3), channel_id=1, source_target_pairs={{0,1},{1,0},{2,3},{3,2},{4,5},{5,4},{6,7},{7,6},{8,9},{9,8},{10,11... | collective-permute-start | bytes 25165832 | tf_op jit(solution)/shard_map/ppermute | solution.py:344
  2.8 20.7 %all-to-all-start = ((s32[128,1,129]{2,1,0:T(1,128)}), s32[128,1,129]{2,1,0:T(1,128)S(1)}, u32[]{:S(2)}, u32[]{:S(2)}) async-start(s32[128,1,129]{2,1,0:T(1,128)} %broadcast_in_dim.98), calls=%async_computation | async-start | bytes 262144 | tf_op jit(solution)/shard_map/all_to_all | solution.py:347
  14.1 10.2 %collective-permute-start.1 = (s32[64,2,256]{2,1,0:T(2,128)}, s32[64,2,256]{2,1,0:T(2,128)S(1)}, u32[]{:S(2)}, u32[]{:S(2)}) collective-permute-start(s32[64,2,256]{2,1,0:T(2,128)} %own_edges.3), channel_id=1, source_target_pairs={{0,1},{1,0},{2,3},{3,2},{4,5},{5,4},{6,7},{7,6},{8,9},{9,8},{10,11... | collective-permute-start | bytes 393224 | tf_op jit(solution)/shard_map/ppermute | solution.py:345
  24.3 0.6 copy-start.2
  32.3 6.1 %copy-start.3 = (s32[4]{0:T(128)S(1)}, s32[4]{0:T(128)}, u32[]{:S(2)}) copy-start(s32[4]{0:T(128)} %fusion.8.where) | copy-start | bytes 52
  32.3 73.1 %all-to-all-start.1 = ((bf16[64,80,512]{2,1,0:T(8,128)(2,1)}), bf16[64,80,512]{2,1,0:T(8,128)(2,1)}, u32[]{:S(2)}, u32[]{:S(2)}) async-start(bf16[64,80,512]{2,1,0:T(8,128)(2,1)} %blend.3.head_ref), calls=%async_computation.1 | async-start | bytes 10485760 | tf_op jit(solution)/shard_map/all_to_all | solution.py:361
  69.2 8.1 %copy-start = (bf16[64,48,512]{2,1,0:T(8,128)(2,1)S(1)}, bf16[64,48,512]{2,1,0:T(8,128)(2,1)}, u32[]{:S(2)}) copy-start(bf16[64,48,512]{2,1,0:T(8,128)(2,1)} %blend.2.tail_ref) | copy-start | bytes 9437188
  71.3 1.4 copy-start.1
  73.5 2.3 %collective-permute-start.2 = (bf16[64,8,512]{2,1,0:T(8,128)(2,1)}, bf16[64,8,512]{2,1,0:T(8,128)(2,1)}, u32[]{:S(2)}, u32[]{:S(2)}) collective-permute-start(bf16[64,8,512]{2,1,0:T(8,128)(2,1)} %fusion.1), channel_id=1, source_target_pairs={{0,1},{1,0},{2,3},{3,2},{4,5},{5,4},{6,7},{7,6},{8,9},{9,8},{10,11... | collective-permute-start | bytes 1572872 | tf_op jit(solution)/shard_map/ppermute | solution.py:385
  105.4 56.5 %all-to-all-start.2 = ((bf16[64,56,512]{2,1,0:T(8,128)(2,1)}), bf16[64,56,512]{2,1,0:T(8,128)(2,1)}, u32[]{:S(2)}, u32[]{:S(2)}) async-start(bf16[64,56,512]{2,1,0:T(8,128)(2,1)} %pad_maximum_fusion), calls=%async_computation.2 | async-start | bytes 7340032 | tf_op jit(solution)/shard_map/all_to_all | solution.py:388

commit v3 on v2

--- a/solution.py
+++ b/solution.py
@@ -18,7 +18,7 @@
 POOL = 8
 MLP_BITS = 3
 HEAD_ROWS = 80
-TAIL_BITS = 3
+TAIL_BITS = 5
 TAIL_GRAPHS = 1 << TAIL_BITS
 MLP = 1 << MLP_BITS
 VMEM_BYTES = 59 * 1024 * 1024

time: 170 us -> 170 us (level)
  no operation moved by 1% of the time
where the time goes in v3:
time: 170 us; the launch traced here: 169 us
  waiting for transfers between devices  73.9 us (43%)
  Pallas kernels  48.3 us (28%)
  starting transfers between devices  25.9 us (15%)
  other arithmetic  11 us (6%)
  local copies, waits for them, and re-layouts  4.61 us (3%)
  between operations  3.49 us (2%)
  matrix products  2.03 us (1%)
    all_to_all x1, waiting for transfers between devices, body(): lax.all_to_all(rest, CHIP, split_axis=0, concat_axis=0, tiled=True)  37.5 us
    all_to_all x1, waiting for transfers between devices, body(): lax.all_to_all(heads, CHIP, split_axis=0, concat_axis=0, tiled=True)  25.6 us
    pallas_call x1, Pallas kernels, pooled_slots(): pl.pallas_call(pool_kernel, out_shape=jax.ShapeDtypeStruct((count, hidden...  18.6 us
    pallas_call x2, Pallas kernels, blended_slots(): pl.pallas_call(functools.partial(blend_kernel, first), out_shape=jax.Shap...  14.2 us
    all_to_all x1, starting transfers between devices, body(): lax.all_to_all(jnp.broadcast_to(info[None], (devices, info.shape[0])), RO...  11.3 us
    all_to_all x1, waiting for transfers between devices, body(): lax.all_to_all(jnp.broadcast_to(info[None], (devices, info.shape[0])), RO...  8.57 us
    all_to_all x1, starting transfers between devices, body(): lax.all_to_all(rest, CHIP, split_axis=0, concat_axis=0, tiled=True)  8.56 us
    pallas_call x1, Pallas kernels, placed_heads(): pl.pallas_call(place_kernel, out_shape=jax.ShapeDtypeStruct((G_DEV, nodes...  8.24 us
  transfers between devices with their start and end apart: 6, of which 4 were waited for; matrix products, arithmetic and copies ran while one was open for 9% of the time, Pallas kernels for 20%

profile of v3, /device:TPU:0, one launch (start us, length us, event | category | flops | bytes accessed | tf_op | source)
XLA Modules:
  0.0 169.3 jit_solution(13238309539654146928)
XLA Ops:
  1.4 0.7 pad_add_fusion
  2.1 0.7 broadcast_in_dim.98
  2.8 11.3 %all-to-all-start = ((s32[128,1,129]{2,1,0:T(1,128)}), s32[128,1,129]{2,1,0:T(1,128)S(1)}, u32[]{:S(2)}, u32[]{:S(2)}) async-start(s32[128,1,129]{2,1,0:T(1,128)} %broadcast_in_dim.98), calls=%async_computation | async-start | bytes 262144 | tf_op jit(solution)/shard_map/all_to_all | solution.py:347
  14.9 8.6 %all-to-all-done = s32[128,1,129]{2,1,0:T(1,128)S(1)} async-done(((s32[128,1,129]{2,1,0:T(1,128)}), s32[128,1,129]{2,1,0:T(1,128)S(1)}, u32[]{:S(2)}, u32[]{:S(2)}) %all-to-all-start) | async-done | bytes 66080 | tf_op jit(solution)/shard_map/all_to_all | solution.py:347
  23.6 0.7 fusion.8.where
  25.0 7.3 %blend.3.head_ref = bf16[64,80,512]{2,1,0:T(8,128)(2,1)} custom-call(s32[4]{0:T(128)} %fusion.8.where, f32[1]{0:T(128)S(6)} %copy.32.scale, bf16[64,128,512]{2,1,0:T(8,128)(2,1)} %own.3, bf16[64,128,512]{2,1,0:T(8,128)(2,1)} %collective-permute-done.par, s32[64,2,256]{2,1,0:T(2,128)} %own_edges.3, s32[64,2,256]{2,1,0:T(2,128)} %copy-done.2), custom_call_target="tpu_custom_call" | custom-call | flops 1006632960 | bytes 16777216 | tf_op jit(solution)/shard_map/blend/pallas_call | solution.py:102
  32.3 5.9 %all-to-all-start.1 = ((bf16[64,80,512]{2,1,0:T(8,128)(2,1)}), bf16[64,80,512]{2,1,0:T(8,128)(2,1)}, u32[]{:S(2)}, u32[]{:S(2)}) async-start(bf16[64,80,512]{2,1,0:T(8,128)(2,1)} %blend.3.head_ref), calls=%async_computation.1 | async-start | bytes 10485760 | tf_op jit(solution)/shard_map/all_to_all | solution.py:361
  38.5 0.6 fusion.13
  40.5 1.3 compare_select_fusion.1
  42.4 0.8 select_reduce_fusion.3
  43.8 6.9 %blend.2.tail_ref = bf16[64,48,512]{2,1,0:T(8,128)(2,1)} custom-call(s32[4]{0:T(128)} %fusion.8.where, f32[1]{0:T(128)S(6)} %copy.32.scale, bf16[64,128,512]{2,1,0:T(8,128)(2,1)} %own.3, bf16[64,128,512]{2,1,0:T(8,128)(2,1)} %collective-permute-done.par, s32[64,2,256]{2,1,0:T(2,128)} %own_edges.3, s32[64,2,256]{2,1,0:T(2,128)} %copy-done.2), custom_call_target="tpu_custom_call" | custom-call | flops 603979776 | bytes 16777216 | tf_op jit(solution)/shard_map/blend/pallas_call | solution.py:102
  50.7 18.6 %pool.1 = f32[64,512]{1,0:T(8,128)} custom-call(s32[64]{0:T(128)} %get-tuple-element.7.counts, bf16[64,80,512]{2,1,0:T(8,128)(2,1)} %blend.3.head_ref, bf16[64,48,512]{2,1,0:T(8,128)(2,1)} %blend.2.tail_ref, bf16[512,512]{1,0:T(8,128)(2,1)} %refs_0_.5, f32[1,512]{1,0:T(1,128)} %bitcast.29, bf16[512,512]{1,0:T(8,128)(2,1)} %refs_2_.5, f32[1,512]{1,0:T(1,128)} %bitcast.32, ...), custom_call_target="tpu_custom_call" | custom-call | flops 12884901888 | bytes 16777216 | tf_op jit(solution)/shard_map/pool/pallas_call | solution.py:165
  69.4 2.0 %fusion.2 = f32[1024,512]{1,0:T(8,128)S(1)} fusion(f32[64,512]{1,0:T(8,128)} %pool.1, s32[64]{0:T(128)S(1)} %broadcast_select_fusion), kind=kOutput, calls=%fused_computation.7 | convolution fusion | flops 402718720 | bytes 2228480 | tf_op jit(solution)/shard_map/dot_general | solution.py:379
  71.4 1.3 copy-done.1
  72.7 0.9 fusion.1
  73.6 2.2 %collective-permute-done.2 = bf16[64,8,512]{2,1,0:T(8,128)(2,1)} collective-permute-done((bf16[64,8,512]{2,1,0:T(8,128)(2,1)}, bf16[64,8,512]{2,1,0:T(8,128)(2,1)}, u32[]{:S(2)}, u32[]{:S(2)}) %collective-permute-start.2) | collective-permute-done | bytes 524320 | tf_op jit(solution)/shard_map/ppermute | solution.py:385
  75.9 1.6 fusion
  77.5 2.1 %pad_maximum_fusion = bf16[64,56,512]{2,1,0:T(8,128)(2,1)} fusion(bf16[64,8,512]{2,1,0:T(8,128)(2,1)S(1)} %fusion, bf16[64,48,512]{2,1,0:T(8,128)(2,1)S(1)} %copy-done), kind=kLoop, calls=%fused_computation | loop fusion | flops 7340032 | bytes 7340032 | tf_op jit(solution)/shard_map/concatenate | solution.py:386
  79.5 25.6 %all-to-all-done.1.arrived = bf16[64,80,512]{2,1,0:T(8,128)(2,1)} async-done(((bf16[64,80,512]{2,1,0:T(8,128)(2,1)}), bf16[64,80,512]{2,1,0:T(8,128)(2,1)}, u32[]{:S(2)}, u32[]{:S(2)}) %all-to-all-start.1) | async-done | bytes 5242912 | tf_op jit(solution)/shard_map/all_to_all | solution.py:361
  105.1 8.6 %all-to-all-start.2 = ((bf16[64,56,512]{2,1,0:T(8,128)(2,1)}), bf16[64,56,512]{2,1,0:T(8,128)(2,1)}, u32[]{:S(2)}, u32[]{:S(2)}) async-start(bf16[64,56,512]{2,1,0:T(8,128)(2,1)} %pad_maximum_fusion), calls=%async_computation.2 | async-start | bytes 7340032 | tf_op jit(solution)/shard_map/all_to_all | solution.py:388
  114.2 1.5 select_reduce_fusion.counts
  116.3 8.2 %place.1.refs_6_ = bf16[32,128,512]{2,1,0:T(8,128)(2,1)} custom-call(s32[32]{0:T(128)} %broadcast_shift-right-arithmetic_fusion.chips, s32[32]{0:T(128)} %select_reduce_fusion.counts, bf16[64,80,512]{2,1,0:T(8,128)(2,1)} %all-to-all-done.1.arrived, bf16[512,512]{1,0:T(8,128)(2,1)} %refs_0_.5, f32[1,512]{1,0:T(1,128)} %bitcast.30, bf16[512,512]{1,0:T(8,128)(2,1)} %refs_2_.5, ...), custom_call_target="tpu_custom_call" | custom-call | flops 4026531840 | bytes 5242880 | tf_op jit(solution)/shard_map/place/pallas_call | solution.py:225
  124.6 37.5 %all-to-all-done.2.arrived = bf16[64,56,512]{2,1,0:T(8,128)(2,1)} async-done(((bf16[64,56,512]{2,1,0:T(8,128)(2,1)}), bf16[64,56,512]{2,1,0:T(8,128)(2,1)}, u32[]{:S(2)}, u32[]{:S(2)}) %all-to-all-start.2) | async-done | bytes 3670048 | tf_op jit(solution)/shard_map/all_to_all | solution.py:388
  162.1 7.2 %finish.1 = (bf16[32,128,512]{2,1,0:T(8,128)(2,1)}, f32[8,512]{1,0:T(8,128)}) custom-call(s32[32]{0:T(128)} %broadcast_shift-right-arithmetic_fusion.chips, s32[32]{0:T(128)} %select_reduce_fusion.counts, bf16[64,56,512]{2,1,0:T(8,128)(2,1)} %all-to-all-done.2.arrived, bf16[512,512]{1,0:T(8,128)(2,1)} %refs_0_.5, ...), custom_call_target="tpu_custom_call", output_to_operand_aliasing={{0}: (9, {})} | custom-call | flops 2415919104 | bytes 3145728 | tf_op jit(solution)/shard_map/finish/pallas_call | solution.py:293
  (33 shorter events, 3.5 us)
Async XLA Ops:
  0.6 23.7 %collective-permute-start = (bf16[64,128,512]{2,1,0:T(8,128)(2,1)}, bf16[64,128,512]{2,1,0:T(8,128)(2,1)}, u32[]{:S(2)}, u32[]{:S(2)}) collective-permute-start(bf16[64,128,512]{2,1,0:T(8,128)(2,1)} %own.3), channel_id=1, source_target_pairs={{0,1},{1,0},{2,3},{3,2},{4,5},{5,4},{6,7},{7,6},{8,9},{9,8},{10,11... | collective-permute-start | bytes 25165832 | tf_op jit(solution)/shard_map/ppermute | solution.py:344
  2.8 20.7 %all-to-all-start = ((s32[128,1,129]{2,1,0:T(1,128)}), s32[128,1,129]{2,1,0:T(1,128)S(1)}, u32[]{:S(2)}, u32[]{:S(2)}) async-start(s32[128,1,129]{2,1,0:T(1,128)} %broadcast_in_dim.98), calls=%async_computation | async-start | bytes 262144 | tf_op jit(solution)/shard_map/all_to_all | solution.py:347
  14.1 10.2 %collective-permute-start.1 = (s32[64,2,256]{2,1,0:T(2,128)}, s32[64,2,256]{2,1,0:T(2,128)S(1)}, u32[]{:S(2)}, u32[]{:S(2)}) collective-permute-start(s32[64,2,256]{2,1,0:T(2,128)} %own_edges.3), channel_id=1, source_target_pairs={{0,1},{1,0},{2,3},{3,2},{4,5},{5,4},{6,7},{7,6},{8,9},{9,8},{10,11... | collective-permute-start | bytes 393224 | tf_op jit(solution)/shard_map/ppermute | solution.py:345
  24.3 0.6 copy-start.2
  32.3 6.2 %copy-start.3 = (s32[4]{0:T(128)S(1)}, s32[4]{0:T(128)}, u32[]{:S(2)}) copy-start(s32[4]{0:T(128)} %fusion.8.where) | copy-start | bytes 52
  32.3 72.8 %all-to-all-start.1 = ((bf16[64,80,512]{2,1,0:T(8,128)(2,1)}), bf16[64,80,512]{2,1,0:T(8,128)(2,1)}, u32[]{:S(2)}, u32[]{:S(2)}) async-start(bf16[64,80,512]{2,1,0:T(8,128)(2,1)} %blend.3.head_ref), calls=%async_computation.1 | async-start | bytes 10485760 | tf_op jit(solution)/shard_map/all_to_all | solution.py:361
  69.4 8.1 %copy-start = (bf16[64,48,512]{2,1,0:T(8,128)(2,1)S(1)}, bf16[64,48,512]{2,1,0:T(8,128)(2,1)}, u32[]{:S(2)}) copy-start(bf16[64,48,512]{2,1,0:T(8,128)(2,1)} %blend.2.tail_ref) | copy-start | bytes 9437188
  71.4 1.4 copy-start.1
  73.6 2.3 %collective-permute-start.2 = (bf16[64,8,512]{2,1,0:T(8,128)(2,1)}, bf16[64,8,512]{2,1,0:T(8,128)(2,1)}, u32[]{:S(2)}, u32[]{:S(2)}) collective-permute-start(bf16[64,8,512]{2,1,0:T(8,128)(2,1)} %fusion.1), channel_id=1, source_target_pairs={{0,1},{1,0},{2,3},{3,2},{4,5},{5,4},{6,7},{7,6},{8,9},{9,8},{10,11... | collective-permute-start | bytes 1572872 | tf_op jit(solution)/shard_map/ppermute | solution.py:385
  105.1 57.0 %all-to-all-start.2 = ((bf16[64,56,512]{2,1,0:T(8,128)(2,1)}), bf16[64,56,512]{2,1,0:T(8,128)(2,1)}, u32[]{:S(2)}, u32[]{:S(2)}) async-start(bf16[64,56,512]{2,1,0:T(8,128)(2,1)} %pad_maximum_fusion), calls=%async_computation.2 | async-start | bytes 7340032 | tf_op jit(solution)/shard_map/all_to_all | solution.py:388

commit v4 on v3

--- a/solution.py
+++ b/solution.py
@@ -18,10 +18,11 @@
 POOL = 8
 MLP_BITS = 3
 HEAD_ROWS = 80
-TAIL_BITS = 5
+TAIL_BITS = 4
 TAIL_GRAPHS = 1 << TAIL_BITS
 MLP = 1 << MLP_BITS
 VMEM_BYTES = 59 * 1024 * 1024
+FINISH_BYTES = 40 * 1024 * 1024
 BLEND_BYTES = 56 * 1024 * 1024
 
 
@@ -307,7 +308,7 @@
             pltpu.SemaphoreType.DMA,
         ],
         input_output_aliases={9: 0},
-        compiler_params=pltpu.CompilerParams(vmem_limit_bytes=VMEM_BYTES),
+        compiler_params=pltpu.CompilerParams(vmem_limit_bytes=FINISH_BYTES),
         cost_estimate=mlp_cost(count * tail, hidden),
         name="finish",
     )(chips, counts, arrived, *weights, node_out)

time: 170 us -> 169 us (level)
  no operation moved by 1% of the time
where the time goes in v4:
time: 169 us
  waiting for transfers between devices  75 us (44%)
  Pallas kernels  48.4 us (29%)
  starting transfers between devices  24.4 us (14%)
  other arithmetic  10.9 us (6%)
  local copies, waits for them, and re-layouts  4.61 us (3%)
  between operations  3.52 us (2%)
  matrix products  2.03 us (1%)
    all_to_all x1, waiting for transfers between devices, body(): lax.all_to_all(rest, CHIP, split_axis=0, concat_axis=0, tiled=True)  37.4 us
    all_to_all x1, waiting for transfers between devices, body(): lax.all_to_all(heads, CHIP, split_axis=0, concat_axis=0, tiled=True)  26.9 us
    pallas_call x1, Pallas kernels, pooled_slots(): pl.pallas_call(pool_kernel, out_shape=jax.ShapeDtypeStruct((count, hidden...  18.6 us
    pallas_call x2, Pallas kernels, blended_slots(): pl.pallas_call(functools.partial(blend_kernel, first), out_shape=jax.Shap...  15.4 us
    all_to_all x1, starting transfers between devices, body(): lax.all_to_all(jnp.broadcast_to(info[None], (devices, info.shape[0])), RO...  11.3 us
    all_to_all x1, waiting for transfers between devices, body(): lax.all_to_all(jnp.broadcast_to(info[None], (devices, info.shape[0])), RO...  8.57 us
    pallas_call x1, Pallas kernels, placed_heads(): pl.pallas_call(place_kernel, out_shape=jax.ShapeDtypeStruct((G_DEV, nodes...  8.32 us
    all_to_all x1, starting transfers between devices, body(): lax.all_to_all(rest, CHIP, split_axis=0, concat_axis=0, tiled=True)  7.19 us
  transfers between devices with their start and end apart: 6, of which 4 were waited for; matrix products, arithmetic and copies ran while one was open for 9% of the time, Pallas kernels for 20%

profile of v4, /device:TPU:0, one launch (start us, length us, event | category | flops | bytes accessed | tf_op | source)
XLA Modules:
  0.0 168.9 jit_solution(13040240391804251883)
XLA Ops:
  1.4 0.7 pad_add_fusion
  2.1 0.7 broadcast_in_dim.98
  2.8 11.3 %all-to-all-start = ((s32[128,1,129]{2,1,0:T(1,128)}), s32[128,1,129]{2,1,0:T(1,128)S(1)}, u32[]{:S(2)}, u32[]{:S(2)}) async-start(s32[128,1,129]{2,1,0:T(1,128)} %broadcast_in_dim.98), calls=%async_computation | async-start | bytes 262144 | tf_op jit(solution)/shard_map/all_to_all | solution.py:348
  14.9 8.6 %all-to-all-done = s32[128,1,129]{2,1,0:T(1,128)S(1)} async-done(((s32[128,1,129]{2,1,0:T(1,128)}), s32[128,1,129]{2,1,0:T(1,128)S(1)}, u32[]{:S(2)}, u32[]{:S(2)}) %all-to-all-start) | async-done | bytes 66080 | tf_op jit(solution)/shard_map/all_to_all | solution.py:348
  23.6 0.7 fusion.8.where
  24.3 0.6 copy-done.10
  25.0 8.0 %blend.3.head_ref = bf16[64,80,512]{2,1,0:T(8,128)(2,1)} custom-call(s32[4]{0:T(128)} %fusion.8.where, f32[1]{0:T(128)S(6)} %copy.32.scale, bf16[64,128,512]{2,1,0:T(8,128)(2,1)} %own.3, bf16[64,128,512]{2,1,0:T(8,128)(2,1)} %collective-permute-done.par, s32[64,2,256]{2,1,0:T(2,128)} %own_edges.3, s32[64,2,256]{2,1,0:T(2,128)} %copy-done.10), custom_call_target="tpu_custom_call" | custom-call | flops 1006632960 | bytes 16777216 | tf_op jit(solution)/shard_map/blend/pallas_call | solution.py:103
  33.0 5.7 %all-to-all-start.1 = ((bf16[64,80,512]{2,1,0:T(8,128)(2,1)}), bf16[64,80,512]{2,1,0:T(8,128)(2,1)}, u32[]{:S(2)}, u32[]{:S(2)}) async-start(bf16[64,80,512]{2,1,0:T(8,128)(2,1)} %blend.3.head_ref), calls=%async_computation.1 | async-start | bytes 10485760 | tf_op jit(solution)/shard_map/all_to_all | solution.py:362
  40.8 1.3 compare_select_fusion.1
  42.7 0.7 select_reduce_fusion.3
  44.1 7.4 %blend.2.tail_ref = bf16[64,48,512]{2,1,0:T(8,128)(2,1)} custom-call(s32[4]{0:T(128)} %fusion.8.where, f32[1]{0:T(128)S(6)} %copy.32.scale, bf16[64,128,512]{2,1,0:T(8,128)(2,1)} %own.3, bf16[64,128,512]{2,1,0:T(8,128)(2,1)} %collective-permute-done.par, s32[64,2,256]{2,1,0:T(2,128)} %own_edges.3, s32[64,2,256]{2,1,0:T(2,128)} %copy-done.10), custom_call_target="tpu_custom_call" | custom-call | flops 603979776 | bytes 16777216 | tf_op jit(solution)/shard_map/blend/pallas_call | solution.py:103
  51.5 18.6 %pool.1 = f32[64,512]{1,0:T(8,128)} custom-call(s32[64]{0:T(128)} %get-tuple-element.7.counts, bf16[64,80,512]{2,1,0:T(8,128)(2,1)} %blend.3.head_ref, bf16[64,48,512]{2,1,0:T(8,128)(2,1)} %blend.2.tail_ref, bf16[512,512]{1,0:T(8,128)(2,1)} %refs_0_.5, f32[1,512]{1,0:T(1,128)} %bitcast.24, bf16[512,512]{1,0:T(8,128)(2,1)} %refs_2_.5, f32[1,512]{1,0:T(1,128)} %bitcast.27, ...), custom_call_target="tpu_custom_call" | custom-call | flops 12884901888 | bytes 16777216 | tf_op jit(solution)/shard_map/pool/pallas_call | solution.py:166
  70.2 2.0 %fusion.2 = f32[1024,512]{1,0:T(8,128)S(1)} fusion(f32[64,512]{1,0:T(8,128)} %pool.1, s32[64]{0:T(128)S(1)} %broadcast_select_fusion), kind=kOutput, calls=%fused_computation.7 | convolution fusion | flops 402718720 | bytes 2228480 | tf_op jit(solution)/shard_map/dot_general | solution.py:380
  72.2 1.3 copy-done.9
  73.6 0.9 fusion.1
  74.5 2.2 %collective-permute-done.2 = bf16[64,8,512]{2,1,0:T(8,128)(2,1)} collective-permute-done((bf16[64,8,512]{2,1,0:T(8,128)(2,1)}, bf16[64,8,512]{2,1,0:T(8,128)(2,1)}, u32[]{:S(2)}, u32[]{:S(2)}) %collective-permute-start.2) | collective-permute-done | bytes 524320 | tf_op jit(solution)/shard_map/ppermute | solution.py:386
  76.7 1.6 fusion
  78.3 2.1 %pad_maximum_fusion = bf16[64,56,512]{2,1,0:T(8,128)(2,1)} fusion(bf16[64,8,512]{2,1,0:T(8,128)(2,1)S(1)} %fusion, bf16[64,48,512]{2,1,0:T(8,128)(2,1)S(1)} %copy-done.8), kind=kLoop, calls=%fused_computation | loop fusion | flops 7340032 | bytes 7340032 | tf_op jit(solution)/shard_map/concatenate | solution.py:387
  80.4 26.9 %all-to-all-done.1.arrived = bf16[64,80,512]{2,1,0:T(8,128)(2,1)} async-done(((bf16[64,80,512]{2,1,0:T(8,128)(2,1)}), bf16[64,80,512]{2,1,0:T(8,128)(2,1)}, u32[]{:S(2)}, u32[]{:S(2)}) %all-to-all-start.1) | async-done | bytes 5242912 | tf_op jit(solution)/shard_map/all_to_all | solution.py:362
  107.3 7.2 %all-to-all-start.2 = ((bf16[64,56,512]{2,1,0:T(8,128)(2,1)}), bf16[64,56,512]{2,1,0:T(8,128)(2,1)}, u32[]{:S(2)}, u32[]{:S(2)}) async-start(bf16[64,56,512]{2,1,0:T(8,128)(2,1)} %pad_maximum_fusion), calls=%async_computation.2 | async-start | bytes 7340032 | tf_op jit(solution)/shard_map/all_to_all | solution.py:389
  115.0 1.6 select_reduce_fusion.counts
  117.1 8.3 %place.1.refs_6_ = bf16[32,128,512]{2,1,0:T(8,128)(2,1)} custom-call(s32[32]{0:T(128)} %broadcast_shift-right-arithmetic_fusion.chips, s32[32]{0:T(128)} %select_reduce_fusion.counts, bf16[64,80,512]{2,1,0:T(8,128)(2,1)} %all-to-all-done.1.arrived, bf16[512,512]{1,0:T(8,128)(2,1)} %refs_0_.5, f32[1,512]{1,0:T(1,128)} %bitcast.25, bf16[512,512]{1,0:T(8,128)(2,1)} %refs_2_.5, ...), custom_call_target="tpu_custom_call" | custom-call | flops 4026531840 | bytes 5242880 | tf_op jit(solution)/shard_map/place/pallas_call | solution.py:226
  125.4 37.4 %all-to-all-done.2.arrived = bf16[64,56,512]{2,1,0:T(8,128)(2,1)} async-done(((bf16[64,56,512]{2,1,0:T(8,128)(2,1)}), bf16[64,56,512]{2,1,0:T(8,128)(2,1)}, u32[]{:S(2)}, u32[]{:S(2)}) %all-to-all-start.2) | async-done | bytes 3670048 | tf_op jit(solution)/shard_map/all_to_all | solution.py:389
  162.9 6.0 %finish.1 = (bf16[32,128,512]{2,1,0:T(8,128)(2,1)}, f32[8,512]{1,0:T(8,128)}) custom-call(s32[32]{0:T(128)S(1)} %copy-done.7, s32[32]{0:T(128)S(1)} %copy-done.6, bf16[64,56,512]{2,1,0:T(8,128)(2,1)} %all-to-all-done.2.arrived, bf16[512,512]{1,0:T(8,128)(2,1)S(1)} %copy-done, f32[1,512]{1,0:T(1,128)S(1)} %bitcast.26, ...), custom_call_target="tpu_custom_call", output_to_operand_aliasing={{0}: (9, {})} | custom-call | flops 2415919104 | bytes 3145728 | tf_op jit(solution)/shard_map/finish/pallas_call | solution.py:294
  (49 shorter events, 3.5 us)
Async XLA Ops:
  0.6 23.7 %collective-permute-start = (bf16[64,128,512]{2,1,0:T(8,128)(2,1)}, bf16[64,128,512]{2,1,0:T(8,128)(2,1)}, u32[]{:S(2)}, u32[]{:S(2)}) collective-permute-start(bf16[64,128,512]{2,1,0:T(8,128)(2,1)} %own.3), channel_id=1, source_target_pairs={{0,1},{1,0},{2,3},{3,2},{4,5},{5,4},{6,7},{7,6},{8,9},{9,8},{10,11... | collective-permute-start | bytes 25165832 | tf_op jit(solution)/shard_map/ppermute | solution.py:345
  2.8 20.7 %all-to-all-start = ((s32[128,1,129]{2,1,0:T(1,128)}), s32[128,1,129]{2,1,0:T(1,128)S(1)}, u32[]{:S(2)}, u32[]{:S(2)}) async-start(s32[128,1,129]{2,1,0:T(1,128)} %broadcast_in_dim.98), calls=%async_computation | async-start | bytes 262144 | tf_op jit(solution)/shard_map/all_to_all | solution.py:348
  14.1 10.2 %collective-permute-start.1 = (s32[64,2,256]{2,1,0:T(2,128)}, s32[64,2,256]{2,1,0:T(2,128)S(1)}, u32[]{:S(2)}, u32[]{:S(2)}) collective-permute-start(s32[64,2,256]{2,1,0:T(2,128)} %own_edges.3), channel_id=1, source_target_pairs={{0,1},{1,0},{2,3},{3,2},{4,5},{5,4},{6,7},{7,6},{8,9},{9,8},{10,11... | collective-permute-start | bytes 393224 | tf_op jit(solution)/shard_map/ppermute | solution.py:346
  24.3 0.7 copy-start.10
  33.0 6.0 %copy-start.11 = (s32[4]{0:T(128)S(1)}, s32[4]{0:T(128)}, u32[]{:S(2)}) copy-start(s32[4]{0:T(128)} %fusion.8.where) | copy-start | bytes 52
  33.0 74.3 %all-to-all-start.1 = ((bf16[64,80,512]{2,1,0:T(8,128)(2,1)}), bf16[64,80,512]{2,1,0:T(8,128)(2,1)}, u32[]{:S(2)}, u32[]{:S(2)}) async-start(bf16[64,80,512]{2,1,0:T(8,128)(2,1)} %blend.3.head_ref), calls=%async_computation.1 | async-start | bytes 10485760 | tf_op jit(solution)/shard_map/all_to_all | solution.py:362
  70.2 8.1 %copy-start.8 = (bf16[64,48,512]{2,1,0:T(8,128)(2,1)S(1)}, bf16[64,48,512]{2,1,0:T(8,128)(2,1)}, u32[]{:S(2)}) copy-start(bf16[64,48,512]{2,1,0:T(8,128)(2,1)} %blend.2.tail_ref) | copy-start | bytes 9437188
  72.2 1.4 copy-start.9
  74.4 2.3 %collective-permute-start.2 = (bf16[64,8,512]{2,1,0:T(8,128)(2,1)}, bf16[64,8,512]{2,1,0:T(8,128)(2,1)}, u32[]{:S(2)}, u32[]{:S(2)}) collective-permute-start(bf16[64,8,512]{2,1,0:T(8,128)(2,1)} %fusion.1), channel_id=1, source_target_pairs={{0,1},{1,0},{2,3},{3,2},{4,5},{5,4},{6,7},{7,6},{8,9},{9,8},{10,11... | collective-permute-start | bytes 1572872 | tf_op jit(solution)/shard_map/ppermute | solution.py:386
  107.3 55.6 %all-to-all-start.2 = ((bf16[64,56,512]{2,1,0:T(8,128)(2,1)}), bf16[64,56,512]{2,1,0:T(8,128)(2,1)}, u32[]{:S(2)}, u32[]{:S(2)}) async-start(bf16[64,56,512]{2,1,0:T(8,128)(2,1)} %pad_maximum_fusion), calls=%async_computation.2 | async-start | bytes 7340032 | tf_op jit(solution)/shard_map/all_to_all | solution.py:389
  117.0 45.8 %copy-start = (bf16[512,512]{1,0:T(8,128)(2,1)S(1)}, bf16[512,512]{1,0:T(8,128)(2,1)}, u32[]{:S(2)}) copy-start(bf16[512,512]{1,0:T(8,128)(2,1)} %refs_0_.5) | copy-start | bytes 1572868
  117.1 45.8 %copy-start.1 = (bf16[512,512]{1,0:T(8,128)(2,1)S(1)}, bf16[512,512]{1,0:T(8,128)(2,1)}, u32[]{:S(2)}) copy-start(bf16[512,512]{1,0:T(8,128)(2,1)} %refs_2_.5) | copy-start | bytes 1572868
  117.1 45.8 %copy-start.2 = (bf16[512,512]{1,0:T(8,128)(2,1)S(1)}, bf16[512,512]{1,0:T(8,128)(2,1)}, u32[]{:S(2)}) copy-start(bf16[512,512]{1,0:T(8,128)(2,1)} %refs_4_.5) | copy-start | bytes 1572868
  117.1 45.8 %copy-start.3 = (f32[512]{0:T(512)S(1)}, f32[512]{0:T(512)}, u32[]{:S(2)}) copy-start(f32[512]{0:T(512)} %param.19) | copy-start | bytes 6148
  117.1 45.8 %copy-start.4 = (f32[512]{0:T(512)S(1)}, f32[512]{0:T(512)}, u32[]{:S(2)}) copy-start(f32[512]{0:T(512)} %param.21) | copy-start | bytes 6148
  117.1 45.8 %copy-start.5 = (f32[512]{0:T(512)S(1)}, f32[512]{0:T(512)}, u32[]{:S(2)}) copy-start(f32[512]{0:T(512)} %param.23) | copy-start | bytes 6148
  117.1 45.8 %copy-start.6 = (s32[32]{0:T(128)S(1)}, s32[32]{0:T(128)}, u32[]{:S(2)}) copy-start(s32[32]{0:T(128)} %select_reduce_fusion.counts) | copy-start | bytes 388
  117.1 45.8 %copy-start.7 = (s32[32]{0:T(128)S(1)}, s32[32]{0:T(128)}, u32[]{:S(2)}) copy-start(s32[32]{0:T(128)} %broadcast_shift-right-arithmetic_fusion.chips) | copy-start | bytes 388

commit v5 on v4

--- a/solution.py
+++ b/solution.py
@@ -30,10 +30,57 @@
     return jnp.sum(jnp.where(keep, values, 0), axis=axis)
 
 
+def info_kernel(live, counts, ids, out):
+    rows, size = out.shape[0], counts.shape[1]
+    for lane, values in ((0, counts), (size, ids)):
+        out[:, :, lane : lane + size] = jnp.broadcast_to(values[...][None], (rows, 1, size))
+    out[:, :, 2 * size :] = jnp.full((rows, 1, 1), live[0], jnp.int32)
+
+
+def info_rows(live, counts, ids, devices):
+    vector = pl.BlockSpec(memory_space=pltpu.VMEM)
+    return pl.pallas_call(
+        info_kernel,
+        out_shape=jax.ShapeDtypeStruct((devices, 1, 2 * counts.shape[1] + 1), jnp.int32),
+        in_specs=[pl.BlockSpec(memory_space=pltpu.SMEM), vector, vector],
+        out_specs=vector,
+        name="info",
+    )(live, counts, ids)
+
+
 def blend_kernel(
-    first, where, scale, own, par, own_edges, par_edges, out, taken, made, taken_sem, made_sem
+    first,
+    where,
+    scale,
+    live,
+    own,
+    par,
+    own_edges_from,
+    par_edges_from,
+    out,
+    taken,
+    made,
+    own_edges,
+    par_edges,
+    taken_sem,
+    made_sem,
+    edge_sem,
 ):
-    core, offset, live_a, live_b = where[0], where[1], where[2], where[3]
+    edge_copies = [
+        pltpu.make_async_copy(own_edges_from, own_edges, edge_sem.at[0]),
+        pltpu.make_async_copy(par_edges_from, par_edges, edge_sem.at[1]),
+    ]
+    for copy in edge_copies:
+        copy.start()
+    chip, core = where[0], where[1]
+    device = lax.broadcasted_iota(jnp.int32, live.shape, 1)
+
+    def total(keep):
+        return jnp.sum(jnp.where(keep, live[...].astype(jnp.float32), 0.0)).astype(jnp.int32)
+
+    offset = total(device < 2 * chip)
+    live_a = total(device == 2 * chip)
+    live_b = total(device == 2 * chip + 1)
     count, nodes, _ = taken.shape
     size = made.shape[1]
     wrap = 2 * count - 1
@@ -63,6 +110,9 @@
     def put(group):
         rows = pl.ds(group * PACK, PACK)
         return pltpu.make_async_copy(made.at[rows], out.at[rows], made_sem.at[group])
+
+    for copy in edge_copies:
+        copy.wait()
 
     @pl.loop(0, count // PACK)
     def _(group):
@@ -95,7 +145,7 @@
         put(group).wait()
 
 
-def blended_slots(own, par, own_edges, par_edges, where, scale, first, size):
+def blended_slots(own, par, own_edges, par_edges, where, live, scale, first, size):
     count, nodes, hidden = own.shape
     anywhere = pl.BlockSpec(memory_space=pl.ANY)
     vector = pl.BlockSpec(memory_space=pltpu.VMEM)
@@ -103,13 +153,16 @@
     return pl.pallas_call(
         functools.partial(blend_kernel, first),
         out_shape=jax.ShapeDtypeStruct((count, size, hidden), jnp.bfloat16),
-        in_specs=[scalar, scalar, anywhere, anywhere, vector, vector],
+        in_specs=[scalar, scalar, vector] + [anywhere] * 4,
         out_specs=anywhere,
         scratch_shapes=[
             pltpu.VMEM((count, nodes, hidden), jnp.bfloat16),
             pltpu.VMEM((count, size, hidden), jnp.bfloat16),
+            pltpu.VMEM(own_edges.shape, jnp.int32),
+            pltpu.VMEM(own_edges.shape, jnp.int32),
             pltpu.SemaphoreType.DMA((count // PACK,)),
             pltpu.SemaphoreType.DMA((count // PACK,)),
+            pltpu.SemaphoreType.DMA((2,)),
         ],
         compiler_params=pltpu.CompilerParams(vmem_limit_bytes=BLEND_BYTES),
         cost_estimate=pl.CostEstimate(
@@ -118,7 +171,7 @@
             transcendentals=0,
         ),
         name="blend",
-    )(where, scale, own, par, own_edges, par_edges)
+    )(where, scale, live, own, par, own_edges, par_edges)
 
 
 def perceptron(rows, weights):
@@ -344,25 +397,22 @@
 
     par_features = lax.ppermute(node_features, "col_2", SWAP)
     par_edges = lax.ppermute(edge_list, "col_2", SWAP)
-    info = jnp.concatenate([live_graphs, node_counts, readout_ids])
-    table = lax.all_to_all(
-        jnp.broadcast_to(info[None], (devices, info.shape[0])), ROW_COL, 0, 0, tiled=True
-    )
-    live = table[:, 0]
-
-    device = lax.broadcasted_iota(jnp.int32, (4, devices), 1)
-    part = lax.broadcasted_iota(jnp.int32, (4, devices), 0)
-    ahead = (part == 1) & (device < 2 * chip)
-    mine = (part >= 2) & (device == 2 * chip + part - 2)
-    own = (part == 0) & (device < core)
-    place = masked_sum(ahead | mine | own, jnp.where(own, 1, live[None, :]), 1)
-
-    graphs = (node_features, par_features, edge_list, par_edges, place, self_weight)
+    info = info_rows(live_graphs, node_counts[None, :], readout_ids[None, :], devices)
+    table = lax.all_to_all(info, ROW_COL, 0, 0, tiled=True)[:, 0]
+    live = table[:, 2 * capacity]
+
+    where = jnp.stack([chip, core])
+    graphs = (node_features, par_features, edge_list, par_edges, where, live[None, :], self_weight)
     heads = blended_slots(*graphs, 0, HEAD_ROWS)
     arrived = lax.all_to_all(heads, CHIP, split_axis=0, concat_axis=0, tiled=True)
     tails = blended_slots(*graphs, HEAD_ROWS, nodes - HEAD_ROWS)
 
-    offset, live_a, live_b = place[1], place[2], place[3]
+    device = lax.broadcasted_iota(jnp.int32, (3, devices), 1)
+    part = lax.broadcasted_iota(jnp.int32, (3, devices), 0)
+    ahead = (part == 0) & (device < 2 * chip)
+    mine = (part >= 1) & (device == 2 * chip + part - 1)
+    sums = masked_sum(ahead | mine, live[None, :], 1)
+    offset, live_a, live_b = sums[0], sums[1], sums[2]
     slot = lax.broadcasted_iota(jnp.int32, (devices // 2,), 0)
     number = (2 * slot + core - offset) & (devices - 1)
     filled = number < live_a + live_b
@@ -370,8 +420,8 @@
     pair = lax.dynamic_slice_in_dim(table, 2 * chip, 2, 0)
     spot = lax.broadcasted_iota(jnp.int32, (devices // 2, 2 * capacity), 1) == picked[:, None]
     spot = spot & filled[:, None]
-    slot_counts = masked_sum(spot, pair[:, 1 : 1 + capacity].reshape(1, -1), 1)
-    slot_ids = masked_sum(spot, pair[:, 1 + capacity :].reshape(1, -1), 1)
+    slot_counts = masked_sum(spot, pair[:, :capacity].reshape(1, -1), 1)
+    slot_ids = masked_sum(spot, pair[:, capacity : 2 * capacity].reshape(1, -1), 1)
     slot_ids = jnp.where(filled, slot_ids, -1)
     pooled = pooled_slots(heads, tails, slot_counts, weights)
     groups = READ_DEV * devices
@@ -400,7 +450,7 @@
     hit = (every[None, :, None] == source[:, None, None]) & (
         lax.broadcasted_iota(jnp.int32, (1, 1, capacity), 2) == source_idx[:, None, None]
     )
-    counts = jnp.sum(jnp.where(hit, table[None, :, 1 : 1 + capacity], 0), axis=(1, 2))
+    counts = jnp.sum(jnp.where(hit, table[None, :, :capacity], 0), axis=(1, 2))
     chips = source >> 1
     node_out = placed_heads(arrived, chips, counts, weights, nodes)
     return tuple(finished(node_out, arrived_rest, chips, counts, weights))

time: 169 us -> 169 us (level)
  transfers between devices with their start and end apart: 6 -> 6, of which waited for: 4 -> 4; matrix products, arithmetic and copies ran while one was open for 9% -> 9% of each run, Pallas kernels for 20% -> 21%
where the time goes in v5:
time: 169 us
  waiting for transfers between devices  74.8 us (44%)
  Pallas kernels  49 us (29%)
  starting transfers between devices  25 us (15%)
  other arithmetic  10 us (6%)
  local copies, waits for them, and re-layouts  4.36 us (3%)
  between operations  3.51 us (2%)
  matrix products  2.02 us (1%)
    all_to_all x1, waiting for transfers between devices, body(): lax.all_to_all(rest, CHIP, split_axis=0, concat_axis=0, tiled=True)  37 us
    all_to_all x1, waiting for transfers between devices, body(): lax.all_to_all(heads, CHIP, split_axis=0, concat_axis=0, tiled=True)  27.8 us
    pallas_call x1, Pallas kernels, pooled_slots(): pl.pallas_call(pool_kernel, out_shape=jax.ShapeDtypeStruct((count, hidden...  18.6 us
    pallas_call x2, Pallas kernels, blended_slots(): pl.pallas_call(functools.partial(blend_kernel, first), out_shape=jax.Shap...  14.6 us
    all_to_all x1, starting transfers between devices, body(): table = lax.all_to_all(info, ROW_COL, 0, 0, tiled=True)[:, 0]  11.3 us
    pallas_call x1, Pallas kernels, placed_heads(): pl.pallas_call(place_kernel, out_shape=jax.ShapeDtypeStruct((G_DEV, nodes...  8.32 us
    all_to_all x1, waiting for transfers between devices, body(): table = lax.all_to_all(info, ROW_COL, 0, 0, tiled=True)[:, 0]  8.02 us
    all_to_all x1, starting transfers between devices, body(): lax.all_to_all(rest, CHIP, split_axis=0, concat_axis=0, tiled=True)  7.46 us
  transfers between devices with their start and end apart: 6, of which 4 were waited for; matrix products, arithmetic and copies ran while one was open for 9% of the time, Pallas kernels for 21%

profile of v5, /device:TPU:0, one launch (start us, length us, event | category | flops | bytes accessed | tf_op | source)
XLA Modules:
  0.0 168.7 jit_solution(7255536751436695100)
XLA Ops:
  1.4 1.4 info.1
  2.8 11.3 %all-to-all-start = ((s32[128,1,129]{2,1,0:T(1,128)}), s32[128,1,129]{2,1,0:T(1,128)S(1)}, u32[]{:S(2)}, u32[]{:S(2)}) async-start(s32[128,1,129]{2,1,0:T(1,128)} %info.1), calls=%async_computation | async-start | bytes 262144 | tf_op jit(solution)/shard_map/all_to_all | solution.py:401
  14.8 0.6 pad_add_fusion.where
  15.4 8.0 %all-to-all-done = s32[128,1,129]{2,1,0:T(1,128)S(1)} async-done(((s32[128,1,129]{2,1,0:T(1,128)}), s32[128,1,129]{2,1,0:T(1,128)S(1)}, u32[]{:S(2)}, u32[]{:S(2)}) %all-to-all-start) | async-done | bytes 66080 | tf_op jit(solution)/shard_map/all_to_all | solution.py:401
  24.1 0.6 copy-done.10
  24.7 7.6 %blend.3.head_ref = bf16[64,80,512]{2,1,0:T(8,128)(2,1)} custom-call(s32[2]{0:T(128)} %pad_add_fusion.where, f32[1]{0:T(128)S(6)} %copy.26.scale, s32[1,128]{1,0:T(1,128)} %get-tuple-element.10.live, bf16[64,128,512]{2,1,0:T(8,128)(2,1)} %own.3, bf16[64,128,512]{2,1,0:T(8,128)(2,1)} %collective-permute-done.par, s32[64,2,256]{2,1,0:T(2,128)} %own_edges_from.3, ...), custom_call_target="tpu_custom_call" | custom-call | flops 1006632960 | bytes 16777216 | tf_op jit(solution)/shard_map/blend/pallas_call | solution.py:153
  32.3 5.7 %all-to-all-start.1 = ((bf16[64,80,512]{2,1,0:T(8,128)(2,1)}), bf16[64,80,512]{2,1,0:T(8,128)(2,1)}, u32[]{:S(2)}, u32[]{:S(2)}) async-start(bf16[64,80,512]{2,1,0:T(8,128)(2,1)} %blend.3.head_ref), calls=%async_computation.1 | async-start | bytes 10485760 | tf_op jit(solution)/shard_map/all_to_all | solution.py:407
  38.5 0.6 fusion.11
  40.4 1.2 compare_select_fusion.1
  42.2 0.7 select_reduce_fusion.3
  43.5 7.0 %blend.2.tail_ref = bf16[64,48,512]{2,1,0:T(8,128)(2,1)} custom-call(s32[2]{0:T(128)} %pad_add_fusion.where, f32[1]{0:T(128)S(6)} %copy.26.scale, s32[1,128]{1,0:T(1,128)} %get-tuple-element.10.live, bf16[64,128,512]{2,1,0:T(8,128)(2,1)} %own.3, bf16[64,128,512]{2,1,0:T(8,128)(2,1)} %collective-permute-done.par, s32[64,2,256]{2,1,0:T(2,128)} %own_edges_from.3, ...), custom_call_target="tpu_custom_call" | custom-call | flops 603979776 | bytes 16777216 | tf_op jit(solution)/shard_map/blend/pallas_call | solution.py:153
  50.5 18.6 %pool.1 = f32[64,512]{1,0:T(8,128)} custom-call(s32[64]{0:T(128)} %get-tuple-element.7.counts, bf16[64,80,512]{2,1,0:T(8,128)(2,1)} %blend.3.head_ref, bf16[64,48,512]{2,1,0:T(8,128)(2,1)} %blend.2.tail_ref, bf16[512,512]{1,0:T(8,128)(2,1)} %refs_0_.5, f32[1,512]{1,0:T(1,128)} %bitcast.30, bf16[512,512]{1,0:T(8,128)(2,1)} %refs_2_.5, f32[1,512]{1,0:T(1,128)} %bitcast.33, ...), custom_call_target="tpu_custom_call" | custom-call | flops 12884901888 | bytes 16777216 | tf_op jit(solution)/shard_map/pool/pallas_call | solution.py:219
  69.2 2.0 %fusion.2 = f32[1024,512]{1,0:T(8,128)S(1)} fusion(f32[64,512]{1,0:T(8,128)} %pool.1, s32[64]{0:T(128)S(1)} %broadcast_select_fusion), kind=kOutput, calls=%fused_computation.7 | convolution fusion | flops 402718720 | bytes 2228480 | tf_op jit(solution)/shard_map/dot_general | solution.py:430
  71.2 1.3 copy-done.9
  72.5 0.9 fusion.1
  73.8 1.9 %collective-permute-done.2 = bf16[64,8,512]{2,1,0:T(8,128)(2,1)} collective-permute-done((bf16[64,8,512]{2,1,0:T(8,128)(2,1)}, bf16[64,8,512]{2,1,0:T(8,128)(2,1)}, u32[]{:S(2)}, u32[]{:S(2)}) %collective-permute-start.2) | collective-permute-done | bytes 524320 | tf_op jit(solution)/shard_map/ppermute | solution.py:436
  75.7 1.6 fusion
  77.2 2.1 %pad_maximum_fusion = bf16[64,56,512]{2,1,0:T(8,128)(2,1)} fusion(bf16[64,8,512]{2,1,0:T(8,128)(2,1)S(1)} %fusion, bf16[64,48,512]{2,1,0:T(8,128)(2,1)S(1)} %copy-done.8), kind=kLoop, calls=%fused_computation | loop fusion | flops 7340032 | bytes 7340032 | tf_op jit(solution)/shard_map/concatenate | solution.py:437
  79.4 27.8 %all-to-all-done.1.arrived = bf16[64,80,512]{2,1,0:T(8,128)(2,1)} async-done(((bf16[64,80,512]{2,1,0:T(8,128)(2,1)}), bf16[64,80,512]{2,1,0:T(8,128)(2,1)}, u32[]{:S(2)}, u32[]{:S(2)}) %all-to-all-start.1) | async-done | bytes 5242912 | tf_op jit(solution)/shard_map/all_to_all | solution.py:407
  107.2 7.5 %all-to-all-start.2 = ((bf16[64,56,512]{2,1,0:T(8,128)(2,1)}), bf16[64,56,512]{2,1,0:T(8,128)(2,1)}, u32[]{:S(2)}, u32[]{:S(2)}) async-start(bf16[64,56,512]{2,1,0:T(8,128)(2,1)} %pad_maximum_fusion), calls=%async_computation.2 | async-start | bytes 7340032 | tf_op jit(solution)/shard_map/all_to_all | solution.py:439
  115.2 1.5 select_reduce_fusion.counts
  117.3 8.3 %place.1.refs_6_ = bf16[32,128,512]{2,1,0:T(8,128)(2,1)} custom-call(s32[32]{0:T(128)} %broadcast_shift-right-arithmetic_fusion.chips, s32[32]{0:T(128)} %select_reduce_fusion.counts, bf16[64,80,512]{2,1,0:T(8,128)(2,1)} %all-to-all-done.1.arrived, bf16[512,512]{1,0:T(8,128)(2,1)} %refs_0_.5, f32[1,512]{1,0:T(1,128)} %bitcast.31, bf16[512,512]{1,0:T(8,128)(2,1)} %refs_2_.5, ...), custom_call_target="tpu_custom_call" | custom-call | flops 4026531840 | bytes 5242880 | tf_op jit(solution)/shard_map/place/pallas_call | solution.py:279
  125.6 37.0 %all-to-all-done.2.arrived = bf16[64,56,512]{2,1,0:T(8,128)(2,1)} async-done(((bf16[64,56,512]{2,1,0:T(8,128)(2,1)}), bf16[64,56,512]{2,1,0:T(8,128)(2,1)}, u32[]{:S(2)}, u32[]{:S(2)}) %all-to-all-start.2) | async-done | bytes 3670048 | tf_op jit(solution)/shard_map/all_to_all | solution.py:439
  162.7 6.0 %finish.1 = (bf16[32,128,512]{2,1,0:T(8,128)(2,1)}, f32[8,512]{1,0:T(8,128)}) custom-call(s32[32]{0:T(128)S(1)} %copy-done.7, s32[32]{0:T(128)S(1)} %copy-done.6, bf16[64,56,512]{2,1,0:T(8,128)(2,1)} %all-to-all-done.2.arrived, bf16[512,512]{1,0:T(8,128)(2,1)S(1)} %copy-done, f32[1,512]{1,0:T(1,128)S(1)} %bitcast.32, ...), custom_call_target="tpu_custom_call", output_to_operand_aliasing={{0}: (9, {})} | custom-call | flops 2415919104 | bytes 3145728 | tf_op jit(solution)/shard_map/finish/pallas_call | solution.py:347
  (46 shorter events, 3.8 us)
Async XLA Ops:
  0.6 23.5 %collective-permute-start = (bf16[64,128,512]{2,1,0:T(8,128)(2,1)}, bf16[64,128,512]{2,1,0:T(8,128)(2,1)}, u32[]{:S(2)}, u32[]{:S(2)}) collective-permute-start(bf16[64,128,512]{2,1,0:T(8,128)(2,1)} %own.3), channel_id=1, source_target_pairs={{0,1},{1,0},{2,3},{3,2},{4,5},{5,4},{6,7},{7,6},{8,9},{9,8},{10,11... | collective-permute-start | bytes 25165832 | tf_op jit(solution)/shard_map/ppermute | solution.py:398
  2.8 20.7 %all-to-all-start = ((s32[128,1,129]{2,1,0:T(1,128)}), s32[128,1,129]{2,1,0:T(1,128)S(1)}, u32[]{:S(2)}, u32[]{:S(2)}) async-start(s32[128,1,129]{2,1,0:T(1,128)} %info.1), calls=%async_computation | async-start | bytes 262144 | tf_op jit(solution)/shard_map/all_to_all | solution.py:401
  14.1 10.0 %collective-permute-start.1 = (s32[64,2,256]{2,1,0:T(2,128)}, s32[64,2,256]{2,1,0:T(2,128)S(1)}, u32[]{:S(2)}, u32[]{:S(2)}) collective-permute-start(s32[64,2,256]{2,1,0:T(2,128)} %own_edges_from.3), channel_id=1, source_target_pairs={{0,1},{1,0},{2,3},{3,2},{4,5},{5,4},{6,7},{7,6},{8,9},{9,8},{10,11... | collective-permute-start | bytes 393224 | tf_op jit(solution)/shard_map/ppermute | solution.py:399
  24.1 0.6 copy-start.10
  32.3 74.9 %all-to-all-start.1 = ((bf16[64,80,512]{2,1,0:T(8,128)(2,1)}), bf16[64,80,512]{2,1,0:T(8,128)(2,1)}, u32[]{:S(2)}, u32[]{:S(2)}) async-start(bf16[64,80,512]{2,1,0:T(8,128)(2,1)} %blend.3.head_ref), calls=%async_computation.1 | async-start | bytes 10485760 | tf_op jit(solution)/shard_map/all_to_all | solution.py:407
  69.2 8.1 %copy-start.8 = (bf16[64,48,512]{2,1,0:T(8,128)(2,1)S(1)}, bf16[64,48,512]{2,1,0:T(8,128)(2,1)}, u32[]{:S(2)}) copy-start(bf16[64,48,512]{2,1,0:T(8,128)(2,1)} %blend.2.tail_ref) | copy-start | bytes 9437188
  71.2 1.3 copy-start.9
  73.4 2.3 %collective-permute-start.2 = (bf16[64,8,512]{2,1,0:T(8,128)(2,1)}, bf16[64,8,512]{2,1,0:T(8,128)(2,1)}, u32[]{:S(2)}, u32[]{:S(2)}) collective-permute-start(bf16[64,8,512]{2,1,0:T(8,128)(2,1)} %fusion.1), channel_id=1, source_target_pairs={{0,1},{1,0},{2,3},{3,2},{4,5},{5,4},{6,7},{7,6},{8,9},{9,8},{10,11... | collective-permute-start | bytes 1572872 | tf_op jit(solution)/shard_map/ppermute | solution.py:436
  107.2 55.4 %all-to-all-start.2 = ((bf16[64,56,512]{2,1,0:T(8,128)(2,1)}), bf16[64,56,512]{2,1,0:T(8,128)(2,1)}, u32[]{:S(2)}, u32[]{:S(2)}) async-start(bf16[64,56,512]{2,1,0:T(8,128)(2,1)} %pad_maximum_fusion), calls=%async_computation.2 | async-start | bytes 7340032 | tf_op jit(solution)/shard_map/all_to_all | solution.py:439
  117.2 45.4 %copy-start = (bf16[512,512]{1,0:T(8,128)(2,1)S(1)}, bf16[512,512]{1,0:T(8,128)(2,1)}, u32[]{:S(2)}) copy-start(bf16[512,512]{1,0:T(8,128)(2,1)} %refs_0_.5) | copy-start | bytes 1572868
  117.2 45.4 %copy-start.1 = (bf16[512,512]{1,0:T(8,128)(2,1)S(1)}, bf16[512,512]{1,0:T(8,128)(2,1)}, u32[]{:S(2)}) copy-start(bf16[512,512]{1,0:T(8,128)(2,1)} %refs_2_.5) | copy-start | bytes 1572868
  117.2 45.4 %copy-start.2 = (bf16[512,512]{1,0:T(8,128)(2,1)S(1)}, bf16[512,512]{1,0:T(8,128)(2,1)}, u32[]{:S(2)}) copy-start(bf16[512,512]{1,0:T(8,128)(2,1)} %refs_4_.5) | copy-start | bytes 1572868
  117.2 45.4 %copy-start.3 = (f32[512]{0:T(512)S(1)}, f32[512]{0:T(512)}, u32[]{:S(2)}) copy-start(f32[512]{0:T(512)} %param.19) | copy-start | bytes 6148
  117.2 45.4 %copy-start.4 = (f32[512]{0:T(512)S(1)}, f32[512]{0:T(512)}, u32[]{:S(2)}) copy-start(f32[512]{0:T(512)} %param.21) | copy-start | bytes 6148
  117.2 45.4 %copy-start.5 = (f32[512]{0:T(512)S(1)}, f32[512]{0:T(512)}, u32[]{:S(2)}) copy-start(f32[512]{0:T(512)} %param.23) | copy-start | bytes 6148
  117.2 45.4 %copy-start.6 = (s32[32]{0:T(128)S(1)}, s32[32]{0:T(128)}, u32[]{:S(2)}) copy-start(s32[32]{0:T(128)} %select_reduce_fusion.counts) | copy-start | bytes 388
  117.2 45.4 %copy-start.7 = (s32[32]{0:T(128)S(1)}, s32[32]{0:T(128)}, u32[]{:S(2)}) copy-start(s32[32]{0:T(128)} %broadcast_shift-right-arithmetic_fusion.chips) | copy-start | bytes 388

commit v6 on v4

--- a/solution.py
+++ b/solution.py
@@ -17,7 +17,7 @@
 PACK = 1 << PACK_BITS
 POOL = 8
 MLP_BITS = 3
-HEAD_ROWS = 80
+HEAD_ROWS = 72
 TAIL_BITS = 4
 TAIL_GRAPHS = 1 << TAIL_BITS
 MLP = 1 << MLP_BITS

time: 169 us -> 168 us (level)
  local copies, waits for them, and re-layouts: 4.61 us -> 2.53 us
    all_to_all x1, waiting for transfers between devices: 37.4 us -> 44.2 us  [body(): lax.all_to_all(rest, CHIP, split_axis=0, concat_axis=0, tiled=True)]
    all_to_all x1, waiting for transfers between devices: 26.9 us -> 21.1 us  [body(): lax.all_to_all(heads, CHIP, split_axis=0, concat_axis=0, tiled=True)]
    concatenate x1, other arithmetic: 2.12 us -> 4.62 us  [body(): rest = jnp.concatenate([tails, both.astype(jnp.bfloat16)], axis=1)]
  transfers between devices with their start and end apart: 6 -> 6, of which waited for: 4 -> 4; matrix products, arithmetic and copies ran while one was open for 9% -> 10% of each run, Pallas kernels for 20% -> 20%
where the time goes in v6:
time: 168 us
  waiting for transfers between devices  75.8 us (45%)
  Pallas kernels  47.3 us (28%)
  starting transfers between devices  24.4 us (15%)
  other arithmetic  12.2 us (7%)
  between operations  3.52 us (2%)
  local copies, waits for them, and re-layouts  2.53 us (2%)
  matrix products  1.88 us (1%)
    all_to_all x1, waiting for transfers between devices, body(): lax.all_to_all(rest, CHIP, split_axis=0, concat_axis=0, tiled=True)  44.2 us
    all_to_all x1, waiting for transfers between devices, body(): lax.all_to_all(heads, CHIP, split_axis=0, concat_axis=0, tiled=True)  21.1 us
    pallas_call x1, Pallas kernels, pooled_slots(): pl.pallas_call(pool_kernel, out_shape=jax.ShapeDtypeStruct((count, hidden...  18.7 us
    pallas_call x2, Pallas kernels, blended_slots(): pl.pallas_call(functools.partial(blend_kernel, first), out_shape=jax.Shap...  14.3 us
    all_to_all x1, starting transfers between devices, body(): lax.all_to_all(jnp.broadcast_to(info[None], (devices, info.shape[0])), RO...  11.3 us
    all_to_all x1, waiting for transfers between devices, body(): lax.all_to_all(jnp.broadcast_to(info[None], (devices, info.shape[0])), RO...  8.57 us
    pallas_call x1, Pallas kernels, placed_heads(): pl.pallas_call(place_kernel, out_shape=jax.ShapeDtypeStruct((G_DEV, nodes...  7.87 us
    all_to_all x1, starting transfers between devices, body(): lax.all_to_all(rest, CHIP, split_axis=0, concat_axis=0, tiled=True)  7.11 us
  transfers between devices with their start and end apart: 6, of which 4 were waited for; matrix products, arithmetic and copies ran while one was open for 10% of the time, Pallas kernels for 20%

profile of v6, /device:TPU:0, one launch (start us, length us, event | category | flops | bytes accessed | tf_op | source)
XLA Modules:
  0.0 167.6 jit_solution(7357713148827956026)
XLA Ops:
  1.4 0.7 pad_add_fusion
  2.1 0.7 broadcast_in_dim.98
  2.8 11.3 %all-to-all-start = ((s32[128,1,129]{2,1,0:T(1,128)}), s32[128,1,129]{2,1,0:T(1,128)S(1)}, u32[]{:S(2)}, u32[]{:S(2)}) async-start(s32[128,1,129]{2,1,0:T(1,128)} %broadcast_in_dim.98), calls=%async_computation | async-start | bytes 262144 | tf_op jit(solution)/shard_map/all_to_all | solution.py:348
  14.9 8.6 %all-to-all-done = s32[128,1,129]{2,1,0:T(1,128)S(1)} async-done(((s32[128,1,129]{2,1,0:T(1,128)}), s32[128,1,129]{2,1,0:T(1,128)S(1)}, u32[]{:S(2)}, u32[]{:S(2)}) %all-to-all-start) | async-done | bytes 66080 | tf_op jit(solution)/shard_map/all_to_all | solution.py:348
  23.6 0.7 fusion.8.where
  24.3 0.7 copy-done.8
  25.0 7.3 %blend.3.head_ref = bf16[64,72,512]{2,1,0:T(8,128)(2,1)} custom-call(s32[4]{0:T(128)} %fusion.8.where, f32[1]{0:T(128)S(6)} %copy.32.scale, bf16[64,128,512]{2,1,0:T(8,128)(2,1)} %own.3, bf16[64,128,512]{2,1,0:T(8,128)(2,1)} %collective-permute-done.par, s32[64,2,256]{2,1,0:T(2,128)} %own_edges.3, s32[64,2,256]{2,1,0:T(2,128)} %copy-done.8), custom_call_target="tpu_custom_call" | custom-call | flops 905969664 | bytes 16777216 | tf_op jit(solution)/shard_map/blend/pallas_call | solution.py:103
  32.3 5.7 %all-to-all-start.1 = ((bf16[64,72,512]{2,1,0:T(8,128)(2,1)}), bf16[64,72,512]{2,1,0:T(8,128)(2,1)}, u32[]{:S(2)}, u32[]{:S(2)}) async-start(bf16[64,72,512]{2,1,0:T(8,128)(2,1)} %blend.3.head_ref), calls=%async_computation.1 | async-start | bytes 9437184 | tf_op jit(solution)/shard_map/all_to_all | solution.py:362
  38.3 0.7 fusion.13
  40.3 1.3 compare_select_fusion.1
  41.6 0.7 broadcast_compare_fusion
  42.3 0.7 select_reduce_fusion.3
  43.0 0.7 broadcast_select_fusion
  43.7 7.0 %blend.2.tail_ref = bf16[64,56,512]{2,1,0:T(8,128)(2,1)} custom-call(s32[4]{0:T(128)} %fusion.8.where, f32[1]{0:T(128)S(6)} %copy.32.scale, bf16[64,128,512]{2,1,0:T(8,128)(2,1)} %own.3, bf16[64,128,512]{2,1,0:T(8,128)(2,1)} %collective-permute-done.par, s32[64,2,256]{2,1,0:T(2,128)} %own_edges.3, s32[64,2,256]{2,1,0:T(2,128)} %copy-done.8), custom_call_target="tpu_custom_call" | custom-call | flops 704643072 | bytes 16777216 | tf_op jit(solution)/shard_map/blend/pallas_call | solution.py:103
  50.7 18.7 %pool.1 = f32[64,512]{1,0:T(8,128)} custom-call(s32[64]{0:T(128)} %get-tuple-element.7.counts, bf16[64,72,512]{2,1,0:T(8,128)(2,1)} %blend.3.head_ref, bf16[64,56,512]{2,1,0:T(8,128)(2,1)} %blend.2.tail_ref, bf16[512,512]{1,0:T(8,128)(2,1)} %refs_0_.5, f32[1,512]{1,0:T(1,128)} %bitcast.24, bf16[512,512]{1,0:T(8,128)(2,1)} %refs_2_.5, f32[1,512]{1,0:T(1,128)} %bitcast.27, ...), custom_call_target="tpu_custom_call" | custom-call | flops 12884901888 | bytes 16777216 | tf_op jit(solution)/shard_map/pool/pallas_call | solution.py:166
  69.3 1.9 %fusion.2 = f32[1024,512]{1,0:T(8,128)S(1)} fusion(f32[64,512]{1,0:T(8,128)} %pool.1, s32[64]{0:T(128)S(1)} %broadcast_select_fusion), kind=kOutput, calls=%fused_computation.7 | convolution fusion | flops 402718720 | bytes 2228480 | tf_op jit(solution)/shard_map/dot_general | solution.py:380
  71.4 1.9 %collective-permute-done.2 = bf16[64,8,512]{2,1,0:T(8,128)(2,1)S(1)} collective-permute-done((bf16[64,8,512]{2,1,0:T(8,128)(2,1)S(1)}, bf16[64,8,512]{2,1,0:T(8,128)(2,1)S(1)}, u32[]{:S(2)}, u32[]{:S(2)}) %collective-permute-start.2) | collective-permute-done | bytes 524320 | tf_op jit(solution)/shard_map/ppermute | solution.py:386
  73.5 4.6 %pad_maximum_fusion = bf16[64,64,512]{2,1,0:T(8,128)(2,1)} fusion(bf16[64,8,512]{2,1,0:T(8,128)(2,1)S(1)} %fusion, bf16[64,56,512]{2,1,0:T(8,128)(2,1)} %blend.2.tail_ref), kind=kLoop, calls=%fused_computation | loop fusion | flops 8388608 | bytes 8388608 | tf_op jit(solution)/shard_map/concatenate | solution.py:387
  78.1 21.1 %all-to-all-done.1.arrived = bf16[64,72,512]{2,1,0:T(8,128)(2,1)} async-done(((bf16[64,72,512]{2,1,0:T(8,128)(2,1)}), bf16[64,72,512]{2,1,0:T(8,128)(2,1)}, u32[]{:S(2)}, u32[]{:S(2)}) %all-to-all-start.1) | async-done | bytes 4718624 | tf_op jit(solution)/shard_map/all_to_all | solution.py:362
  99.2 7.1 %all-to-all-start.2 = ((bf16[64,64,512]{2,1,0:T(8,128)(2,1)}), bf16[64,64,512]{2,1,0:T(8,128)(2,1)}, u32[]{:S(2)}, u32[]{:S(2)}) async-start(bf16[64,64,512]{2,1,0:T(8,128)(2,1)} %pad_maximum_fusion), calls=%async_computation.2 | async-start | bytes 8388608 | tf_op jit(solution)/shard_map/all_to_all | solution.py:389
  106.8 1.6 select_reduce_fusion.counts
  109.0 7.9 %place.1.refs_6_ = bf16[32,128,512]{2,1,0:T(8,128)(2,1)} custom-call(s32[32]{0:T(128)} %broadcast_shift-right-arithmetic_fusion.chips, s32[32]{0:T(128)} %select_reduce_fusion.counts, bf16[64,72,512]{2,1,0:T(8,128)(2,1)} %all-to-all-done.1.arrived, bf16[512,512]{1,0:T(8,128)(2,1)} %refs_0_.5, f32[1,512]{1,0:T(1,128)} %bitcast.25, bf16[512,512]{1,0:T(8,128)(2,1)} %refs_2_.5, ...), custom_call_target="tpu_custom_call" | custom-call | flops 3623878656 | bytes 4718592 | tf_op jit(solution)/shard_map/place/pallas_call | solution.py:226
  116.9 44.2 %all-to-all-done.2.arrived = bf16[64,64,512]{2,1,0:T(8,128)(2,1)} async-done(((bf16[64,64,512]{2,1,0:T(8,128)(2,1)}), bf16[64,64,512]{2,1,0:T(8,128)(2,1)}, u32[]{:S(2)}, u32[]{:S(2)}) %all-to-all-start.2) | async-done | bytes 4194336 | tf_op jit(solution)/shard_map/all_to_all | solution.py:389
  161.1 6.5 %finish.1 = (bf16[32,128,512]{2,1,0:T(8,128)(2,1)}, f32[8,512]{1,0:T(8,128)}) custom-call(s32[32]{0:T(128)S(1)} %copy-done.7, s32[32]{0:T(128)S(1)} %copy-done, bf16[64,64,512]{2,1,0:T(8,128)(2,1)} %all-to-all-done.2.arrived, bf16[512,512]{1,0:T(8,128)(2,1)S(1)} %copy-done.1, f32[1,512]{1,0:T(1,128)S(1)} %bitcast.26, ...), custom_call_target="tpu_custom_call", output_to_operand_aliasing={{0}: (9, {})} | custom-call | flops 2818572288 | bytes 3670016 | tf_op jit(solution)/shard_map/finish/pallas_call | solution.py:294
  (45 shorter events, 1.9 us)
Async XLA Ops:
  0.6 23.7 %collective-permute-start = (bf16[64,128,512]{2,1,0:T(8,128)(2,1)}, bf16[64,128,512]{2,1,0:T(8,128)(2,1)}, u32[]{:S(2)}, u32[]{:S(2)}) collective-permute-start(bf16[64,128,512]{2,1,0:T(8,128)(2,1)} %own.3), channel_id=1, source_target_pairs={{0,1},{1,0},{2,3},{3,2},{4,5},{5,4},{6,7},{7,6},{8,9},{9,8},{10,11... | collective-permute-start | bytes 25165832 | tf_op jit(solution)/shard_map/ppermute | solution.py:345
  2.8 20.7 %all-to-all-start = ((s32[128,1,129]{2,1,0:T(1,128)}), s32[128,1,129]{2,1,0:T(1,128)S(1)}, u32[]{:S(2)}, u32[]{:S(2)}) async-start(s32[128,1,129]{2,1,0:T(1,128)} %broadcast_in_dim.98), calls=%async_computation | async-start | bytes 262144 | tf_op jit(solution)/shard_map/all_to_all | solution.py:348
  14.1 10.2 %collective-permute-start.1 = (s32[64,2,256]{2,1,0:T(2,128)}, s32[64,2,256]{2,1,0:T(2,128)S(1)}, u32[]{:S(2)}, u32[]{:S(2)}) collective-permute-start(s32[64,2,256]{2,1,0:T(2,128)} %own_edges.3), channel_id=1, source_target_pairs={{0,1},{1,0},{2,3},{3,2},{4,5},{5,4},{6,7},{7,6},{8,9},{9,8},{10,11... | collective-permute-start | bytes 393224 | tf_op jit(solution)/shard_map/ppermute | solution.py:346
  24.3 0.7 copy-start.8
  32.3 6.0 %copy-start.9 = (s32[4]{0:T(128)S(1)}, s32[4]{0:T(128)}, u32[]{:S(2)}) copy-start(s32[4]{0:T(128)} %fusion.8.where) | copy-start | bytes 52
  32.3 66.9 %all-to-all-start.1 = ((bf16[64,72,512]{2,1,0:T(8,128)(2,1)}), bf16[64,72,512]{2,1,0:T(8,128)(2,1)}, u32[]{:S(2)}, u32[]{:S(2)}) async-start(bf16[64,72,512]{2,1,0:T(8,128)(2,1)} %blend.3.head_ref), calls=%async_computation.1 | async-start | bytes 9437184 | tf_op jit(solution)/shard_map/all_to_all | solution.py:362
  71.3 2.0 %collective-permute-start.2 = (bf16[64,8,512]{2,1,0:T(8,128)(2,1)S(1)}, bf16[64,8,512]{2,1,0:T(8,128)(2,1)S(1)}, u32[]{:S(2)}, u32[]{:S(2)}) collective-permute-start(bf16[64,8,512]{2,1,0:T(8,128)(2,1)S(1)} %fusion.1), channel_id=1, source_target_pairs={{0,1},{1,0},{2,3},{3,2},{4,5},{5,4},{6,7},{7,6},{8,9},{9,8},{10,11... | collective-permute-start | bytes 1572872 | tf_op jit(solution)/shard_map/ppermute | solution.py:386
  99.2 61.8 %all-to-all-start.2 = ((bf16[64,64,512]{2,1,0:T(8,128)(2,1)}), bf16[64,64,512]{2,1,0:T(8,128)(2,1)}, u32[]{:S(2)}, u32[]{:S(2)}) async-start(bf16[64,64,512]{2,1,0:T(8,128)(2,1)} %pad_maximum_fusion), calls=%async_computation.2 | async-start | bytes 8388608 | tf_op jit(solution)/shard_map/all_to_all | solution.py:389
  108.9 52.1 %copy-start = (s32[32]{0:T(128)S(1)}, s32[32]{0:T(128)}, u32[]{:S(2)}) copy-start(s32[32]{0:T(128)} %select_reduce_fusion.counts) | copy-start | bytes 388
  108.9 52.1 %copy-start.1 = (bf16[512,512]{1,0:T(8,128)(2,1)S(1)}, bf16[512,512]{1,0:T(8,128)(2,1)}, u32[]{:S(2)}) copy-start(bf16[512,512]{1,0:T(8,128)(2,1)} %refs_0_.5) | copy-start | bytes 1572868
  108.9 52.1 %copy-start.2 = (bf16[512,512]{1,0:T(8,128)(2,1)S(1)}, bf16[512,512]{1,0:T(8,128)(2,1)}, u32[]{:S(2)}) copy-start(bf16[512,512]{1,0:T(8,128)(2,1)} %refs_2_.5) | copy-start | bytes 1572868
  108.9 52.1 %copy-start.3 = (bf16[512,512]{1,0:T(8,128)(2,1)S(1)}, bf16[512,512]{1,0:T(8,128)(2,1)}, u32[]{:S(2)}) copy-start(bf16[512,512]{1,0:T(8,128)(2,1)} %refs_4_.5) | copy-start | bytes 1572868
  108.9 52.1 %copy-start.4 = (f32[512]{0:T(512)S(1)}, f32[512]{0:T(512)}, u32[]{:S(2)}) copy-start(f32[512]{0:T(512)} %param.19) | copy-start | bytes 6148
  109.0 52.1 %copy-start.5 = (f32[512]{0:T(512)S(1)}, f32[512]{0:T(512)}, u32[]{:S(2)}) copy-start(f32[512]{0:T(512)} %param.21) | copy-start | bytes 6148
  109.0 52.1 %copy-start.6 = (f32[512]{0:T(512)S(1)}, f32[512]{0:T(512)}, u32[]{:S(2)}) copy-start(f32[512]{0:T(512)} %param.23) | copy-start | bytes 6148
  109.0 52.1 %copy-start.7 = (s32[32]{0:T(128)S(1)}, s32[32]{0:T(128)}, u32[]{:S(2)}) copy-start(s32[32]{0:T(128)} %broadcast_shift-right-arithmetic_fusion.chips) | copy-start | bytes 388
